TPU v7x, 128 devices: a whole 4x4x4 slice. The times are simulated.
128 devices in a mesh: sys: 1, aux: 16 (over z, y), orb: 8 (over x, core).
Axes of the slice: x: 4, y: 4, z: 4, core: 2. Of those that a mesh axis runs over, the one named last changes fastest.
Arguments:
- b_tensor: float32 [1152, 448, 448], P(('sys', 'aux'), 'orb')
- c_alpha: float32 [448, 39], P('sys')
- c_beta: float32 [448, 38], P('sys')
Outputs:
- output 1: float32 [448, 448], P(('sys', 'orb'), 'aux')
- output 2: float32 [448, 448], P(('sys', 'orb'), 'aux')
All inputs are finite; a program needn't handle non-finite values.
Results may differ from a plain program's by a relative error of at most 0.001.
Values are sent between devices in bfloat16 or wider.
A program may use at most 1 GiB of HBM per device.

v0:
```python
import jax
import jax.numpy as jnp
from jax import lax
from jax.sharding import PartitionSpec as P

TOP_PRECISION = lax.Precision.HIGHEST


def solution(mesh):
    orb_count = mesh.shape['orb']
    shift_pairs = [(source, (source + 1) % orb_count) for source in range(orb_count)]

    def pair_product(left, right):
        return jnp.einsum('qmi,qni->mn', left, right, precision=TOP_PRECISION, preferred_element_type=jnp.float32)

    def local_build(b_local, c_alpha, c_beta):
        m_loc = b_local.shape[1]
        n_bas = b_local.shape[2]
        orb_index = lax.axis_index('orb')
        row_start = orb_index * m_loc
        alpha_rows = lax.dynamic_slice_in_dim(c_alpha, row_start, m_loc, 0)
        beta_rows = lax.dynamic_slice_in_dim(c_beta, row_start, m_loc, 0)
        dens_rows = jnp.einsum('mi,si->ms', alpha_rows, c_alpha, precision=TOP_PRECISION, preferred_element_type=jnp.float32) + jnp.einsum('mi,si->ms', beta_rows, c_beta, precision=TOP_PRECISION, preferred_element_type=jnp.float32)
        gamma_part = jnp.einsum('qms,ms->q', b_local, dens_rows, precision=TOP_PRECISION, preferred_element_type=jnp.float32)
        gamma_vec = lax.psum(gamma_part, 'orb')
        coul_part = jnp.einsum('qmn,q->mn', b_local, gamma_vec, precision=TOP_PRECISION, preferred_element_type=jnp.float32)
        half_alpha = jnp.einsum('qml,li->qmi', b_local, c_alpha, precision=TOP_PRECISION, preferred_element_type=jnp.float32)
        half_beta = jnp.einsum('qml,li->qmi', b_local, c_beta, precision=TOP_PRECISION, preferred_element_type=jnp.float32)
        empty_rows = jnp.zeros((m_loc, n_bas), jnp.float32)
        exch_alpha = lax.dynamic_update_slice_in_dim(empty_rows, pair_product(half_alpha, half_alpha), row_start, 1)
        exch_beta = lax.dynamic_update_slice_in_dim(empty_rows, pair_product(half_beta, half_beta), row_start, 1)

        def pass_step(step, carry):
            visit_alpha, visit_beta, acc_alpha, acc_beta = carry
            visit_alpha = lax.ppermute(visit_alpha, 'orb', shift_pairs)
            visit_beta = lax.ppermute(visit_beta, 'orb', shift_pairs)
            col_start = ((orb_index - step) % orb_count) * m_loc
            acc_alpha = lax.dynamic_update_slice_in_dim(acc_alpha, pair_product(half_alpha, visit_alpha), col_start, 1)
            acc_beta = lax.dynamic_update_slice_in_dim(acc_beta, pair_product(half_beta, visit_beta), col_start, 1)
            return visit_alpha, visit_beta, acc_alpha, acc_beta

        loop_out = lax.fori_loop(1, orb_count, pass_step, (half_alpha, half_beta, exch_alpha, exch_beta))
        g_alpha = lax.psum_scatter(coul_part - loop_out[2], 'aux', scatter_dimension=1, tiled=True)
        g_beta = lax.psum_scatter(coul_part - loop_out[3], 'aux', scatter_dimension=1, tiled=True)
        return g_alpha, g_beta

    spec_b = P(('sys', 'aux'), 'orb', None)
    spec_c = P('sys', None)
    spec_g = P(('sys', 'orb'), 'aux')
    return jax.shard_map(local_build, mesh=mesh, in_specs=(spec_b, spec_c, spec_c), out_specs=(spec_g, spec_g), check_vma=False)
```

profile of v0, /device:TPU:88, one launch (start us, length us, event | category | flops | bytes accessed | tf_op | source)
XLA Modules:
  0.0 362.2 jit_solution(15789201008533663932)
XLA Ops:
  1.5 14.8 %fusion.13 = f32[72,56,39]{1,2,0:T(8,128)S(1)} fusion(f32[72,56,448]{2,1,0:T(8,128)} %param.5, f32[448,39]{0,1:T(8,128)S(1)} %copy-done), kind=kOutput, calls=%fused_computation.16 | convolution fusion | flops 845365248 | bytes 7924224 | tf_op jit(solution)/shard_map/qml,li->qmi/dot_general | solution.py:27
  19.8 15.0 %fusion.11 = f32[72,56,38]{1,2,0:T(8,128)S(1)} fusion(f32[72,56,448]{2,1,0:T(8,128)} %param.5, f32[448,38]{0,1:T(8,128)S(1)} %copy-done.1), kind=kOutput, calls=%fused_computation.14 | convolution fusion | flops 823689216 | bytes 7906304 | tf_op jit(solution)/shard_map/qml,li->qmi/dot_general | solution.py:28
  46.6 220.7 %while.21 = (s32[]{:T(128)}, f32[72,56,39]{0,1,2:T(8,128)}, f32[72,56,38]{0,1,2:T(8,128)}, f32[56,448]{1,0:T(8,128)}, f32[56,448]{1,0:T(8,128)}, /*index=5*/f32[...) while((s32[]{:T(128)}, f32[72,56,39]{0,1,2:T(8,128)}, ...), condition=%wide.region_2.3_spmd, body=%wide.region_1.2_spmd.sunk | while | flops 208631808 | bytes 10010500 | solution.py:42
  48.5 13.9 %collective-permute-done.1 = f32[72,56,38]{0,1,2:T(8,128)S(1)} collective-permute-done((f32[72,56,38]{0,1,2:T(8,128)}, f32[72,56,38]{0,1,2:T(8,128)S(1)}, u32[]{:S(2)}, u32[]{:S(2)}) %collective-permute-start.1) | collective-permute-done | bytes 612896 | tf_op jit(solution)/shard_map/while/body/eval_jaxpr/ppermute | solution.py:36
  67.3 7.2 %collective-permute-done = f32[72,56,39]{0,1,2:T(8,128)S(1)} collective-permute-done((f32[72,56,39]{0,1,2:T(8,128)}, f32[72,56,39]{0,1,2:T(8,128)S(1)}, u32[]{:S(2)}, u32[]{:S(2)}) %collective-permute-start) | collective-permute-done | bytes 629024 | tf_op jit(solution)/shard_map/while/body/eval_jaxpr/ppermute | solution.py:35
  78.9 15.0 %collective-permute-done.1 = f32[72,56,38]{0,1,2:T(8,128)S(1)} collective-permute-done((f32[72,56,38]{0,1,2:T(8,128)}, f32[72,56,38]{0,1,2:T(8,128)S(1)}, u32[]{:S(2)}, u32[]{:S(2)}) %collective-permute-start.1) | collective-permute-done | bytes 612896 | tf_op jit(solution)/shard_map/while/body/eval_jaxpr/ppermute | solution.py:36
  98.8 7.1 %collective-permute-done = f32[72,56,39]{0,1,2:T(8,128)S(1)} collective-permute-done((f32[72,56,39]{0,1,2:T(8,128)}, f32[72,56,39]{0,1,2:T(8,128)S(1)}, u32[]{:S(2)}, u32[]{:S(2)}) %collective-permute-start) | collective-permute-done | bytes 629024 | tf_op jit(solution)/shard_map/while/body/eval_jaxpr/ppermute | solution.py:35
  109.6 15.9 %collective-permute-done.1 = f32[72,56,38]{0,1,2:T(8,128)S(1)} collective-permute-done((f32[72,56,38]{0,1,2:T(8,128)}, f32[72,56,38]{0,1,2:T(8,128)S(1)}, u32[]{:S(2)}, u32[]{:S(2)}) %collective-permute-start.1) | collective-permute-done | bytes 612896 | tf_op jit(solution)/shard_map/while/body/eval_jaxpr/ppermute | solution.py:36
  130.3 7.1 %collective-permute-done = f32[72,56,39]{0,1,2:T(8,128)S(1)} collective-permute-done((f32[72,56,39]{0,1,2:T(8,128)}, f32[72,56,39]{0,1,2:T(8,128)S(1)}, u32[]{:S(2)}, u32[]{:S(2)}) %collective-permute-start) | collective-permute-done | bytes 629024 | tf_op jit(solution)/shard_map/while/body/eval_jaxpr/ppermute | solution.py:35
  141.1 15.9 %collective-permute-done.1 = f32[72,56,38]{0,1,2:T(8,128)S(1)} collective-permute-done((f32[72,56,38]{0,1,2:T(8,128)}, f32[72,56,38]{0,1,2:T(8,128)S(1)}, u32[]{:S(2)}, u32[]{:S(2)}) %collective-permute-start.1) | collective-permute-done | bytes 612896 | tf_op jit(solution)/shard_map/while/body/eval_jaxpr/ppermute | solution.py:36
  161.9 7.1 %collective-permute-done = f32[72,56,39]{0,1,2:T(8,128)S(1)} collective-permute-done((f32[72,56,39]{0,1,2:T(8,128)}, f32[72,56,39]{0,1,2:T(8,128)S(1)}, u32[]{:S(2)}, u32[]{:S(2)}) %collective-permute-start) | collective-permute-done | bytes 629024 | tf_op jit(solution)/shard_map/while/body/eval_jaxpr/ppermute | solution.py:35
  172.7 15.9 %collective-permute-done.1 = f32[72,56,38]{0,1,2:T(8,128)S(1)} collective-permute-done((f32[72,56,38]{0,1,2:T(8,128)}, f32[72,56,38]{0,1,2:T(8,128)S(1)}, u32[]{:S(2)}, u32[]{:S(2)}) %collective-permute-start.1) | collective-permute-done | bytes 612896 | tf_op jit(solution)/shard_map/while/body/eval_jaxpr/ppermute | solution.py:36
  193.4 7.1 %collective-permute-done = f32[72,56,39]{0,1,2:T(8,128)S(1)} collective-permute-done((f32[72,56,39]{0,1,2:T(8,128)}, f32[72,56,39]{0,1,2:T(8,128)S(1)}, u32[]{:S(2)}, u32[]{:S(2)}) %collective-permute-start) | collective-permute-done | bytes 629024 | tf_op jit(solution)/shard_map/while/body/eval_jaxpr/ppermute | solution.py:35
  204.2 15.9 %collective-permute-done.1 = f32[72,56,38]{0,1,2:T(8,128)S(1)} collective-permute-done((f32[72,56,38]{0,1,2:T(8,128)}, f32[72,56,38]{0,1,2:T(8,128)S(1)}, u32[]{:S(2)}, u32[]{:S(2)}) %collective-permute-start.1) | collective-permute-done | bytes 612896 | tf_op jit(solution)/shard_map/while/body/eval_jaxpr/ppermute | solution.py:36
  225.0 7.1 %collective-permute-done = f32[72,56,39]{0,1,2:T(8,128)S(1)} collective-permute-done((f32[72,56,39]{0,1,2:T(8,128)}, f32[72,56,39]{0,1,2:T(8,128)S(1)}, u32[]{:S(2)}, u32[]{:S(2)}) %collective-permute-start) | collective-permute-done | bytes 629024 | tf_op jit(solution)/shard_map/while/body/eval_jaxpr/ppermute | solution.py:35
  235.8 15.9 %collective-permute-done.1 = f32[72,56,38]{0,1,2:T(8,128)S(1)} collective-permute-done((f32[72,56,38]{0,1,2:T(8,128)}, f32[72,56,38]{0,1,2:T(8,128)S(1)}, u32[]{:S(2)}, u32[]{:S(2)}) %collective-permute-start.1) | collective-permute-done | bytes 612896 | tf_op jit(solution)/shard_map/while/body/eval_jaxpr/ppermute | solution.py:36
  256.5 7.1 %collective-permute-done = f32[72,56,39]{0,1,2:T(8,128)S(1)} collective-permute-done((f32[72,56,39]{0,1,2:T(8,128)}, f32[72,56,39]{0,1,2:T(8,128)S(1)}, u32[]{:S(2)}, u32[]{:S(2)}) %collective-permute-start) | collective-permute-done | bytes 629024 | tf_op jit(solution)/shard_map/while/body/eval_jaxpr/ppermute | solution.py:35
  270.7 11.0 %fusion.7 = f32[72]{0:T(128)S(1)} fusion(f32[72,56,448]{2,1,0:T(8,128)} %param.5, f32[56,448,1]{1,0,2:T(8,128)S(1)} %fusion.6), kind=kOutput, calls=%fused_computation.10 | convolution fusion | flops 21676032 | bytes 7325984 | tf_op jit(solution)/shard_map/qms,ms->q/dot_general | solution.py:24
  281.8 12.6 %psum.7 = f32[72]{0:T(128)S(1)} all-reduce(f32[72]{0:T(128)S(1)} %fusion.7), channel_id=1, replica_groups=mesh['sys'=1,'aux'=16,'orb'=8] {'orb'}, use_global_device_ids=true, to_apply=%region_0.0 | all-reduce | flops 72 | bytes 576 | tf_op jit(solution)/shard_map/psum | solution.py:25
  294.4 9.9 %fusion.2 = f32[1,56,448]{2,0,1:T(1,128)S(1)} fusion(f32[72,56,448]{2,1,0:T(8,128)} %param.5, f32[72]{0:T(128)S(1)} %psum.7), kind=kOutput, calls=%fused_computation.2 | convolution fusion | flops 21676032 | bytes 7325984 | tf_op jit(solution)/shard_map/qmn,q->mn/dot_general | solution.py:26
  304.5 33.5 %fusion.21 = (f32[56,32]{0,1:T(8,128)S(1)}, f32[56,32]{0,1:T(8,128)S(1)}) fusion(f32[56,448]{0,1:T(8,128)S(1)} %get-tuple-element.241, f32[56,448]{0,1:T(8,128)S(1)} %get-tuple-element.240), kind=kCustom, calls=%all-reduce-scatter.2 | all-reduce-scatter fusion | flops 57345 | bytes 215552
  338.0 6.3 %collective-permute-start.4 = (f32[56,32]{0,1:T(8,128)S(1)}, f32[56,32]{0,1:T(8,128)S(1)}, u32[]{:S(2)}, u32[]{:S(2)}) collective-permute-start(f32[56,32]{0,1:T(8,128)S(1)} %get-tuple-element.239), channel_id=1, source_target_pairs={{0,8},{8,16},{16,24},{24,32},{32,40},{40,48},{48,56},{56,64},{64,7... | collective-permute-start | bytes 21512
  344.4 4.2 %collective-permute-start.5 = (f32[56,28]{0,1:T(8,128)S(1)}, f32[56,28]{0,1:T(8,128)S(1)}, u32[]{:S(2)}, u32[]{:S(2)}) collective-permute-start(f32[56,28]{0,1:T(8,128)S(1)} %slice.1), channel_id=1, source_target_pairs={{0,16},{8,24},{16,32},{24,40},{32,48},{40,56},{48,64},{56,72},{64,... | collective-permute-start | bytes 18824
  348.6 5.5 %collective-permute-start.2 = (f32[56,32]{0,1:T(8,128)S(1)}, f32[56,32]{0,1:T(8,128)S(1)}, u32[]{:S(2)}, u32[]{:S(2)}) collective-permute-start(f32[56,32]{0,1:T(8,128)S(1)} %get-tuple-element.238), channel_id=1, source_target_pairs={{0,8},{8,16},{16,24},{24,32},{32,40},{40,48},{48,56},{56,64},{64,7... | collective-permute-start | bytes 21512
  (90 shorter events, 89.4 us)
Async XLA Ops:
  0.6 0.9 copy-start
  18.9 0.9 copy-start.1
  46.6 15.9 %collective-permute-start.1 = (f32[72,56,38]{0,1,2:T(8,128)}, f32[72,56,38]{0,1,2:T(8,128)S(1)}, u32[]{:S(2)}, u32[]{:S(2)}) collective-permute-start(f32[72,56,38]{0,1,2:T(8,128)} %get-tuple-element.307), channel_id=1, source_target_pairs={{0,1},{1,2},{2,3},{3,4},{4,5},{5,6},{6,7},{7,0},{8,9},{9,10},{10,1... | collective-permute-start | bytes 1838600 | tf_op jit(solution)/shard_map/while/body/eval_jaxpr/ppermute | solution.py:36
  46.8 27.7 %collective-permute-start = (f32[72,56,39]{0,1,2:T(8,128)}, f32[72,56,39]{0,1,2:T(8,128)S(1)}, u32[]{:S(2)}, u32[]{:S(2)}) collective-permute-start(f32[72,56,39]{0,1,2:T(8,128)} %get-tuple-element.306), channel_id=1, source_target_pairs={{0,1},{1,2},{2,3},{3,4},{4,5},{5,6},{6,7},{7,0},{8,9},{9,10},{10,1... | collective-permute-start | bytes 1886984 | tf_op jit(solution)/shard_map/while/body/eval_jaxpr/ppermute | solution.py:35
  78.0 15.9 %collective-permute-start.1 = (f32[72,56,38]{0,1,2:T(8,128)}, f32[72,56,38]{0,1,2:T(8,128)S(1)}, u32[]{:S(2)}, u32[]{:S(2)}) collective-permute-start(f32[72,56,38]{0,1,2:T(8,128)} %get-tuple-element.307), channel_id=1, source_target_pairs={{0,1},{1,2},{2,3},{3,4},{4,5},{5,6},{6,7},{7,0},{8,9},{9,10},{10,1... | collective-permute-start | bytes 1838600 | tf_op jit(solution)/shard_map/while/body/eval_jaxpr/ppermute | solution.py:36
  78.0 27.9 %collective-permute-start = (f32[72,56,39]{0,1,2:T(8,128)}, f32[72,56,39]{0,1,2:T(8,128)S(1)}, u32[]{:S(2)}, u32[]{:S(2)}) collective-permute-start(f32[72,56,39]{0,1,2:T(8,128)} %get-tuple-element.306), channel_id=1, source_target_pairs={{0,1},{1,2},{2,3},{3,4},{4,5},{5,6},{6,7},{7,0},{8,9},{9,10},{10,1... | collective-permute-start | bytes 1886984 | tf_op jit(solution)/shard_map/while/body/eval_jaxpr/ppermute | solution.py:35
  109.6 15.9 %collective-permute-start.1 = (f32[72,56,38]{0,1,2:T(8,128)}, f32[72,56,38]{0,1,2:T(8,128)S(1)}, u32[]{:S(2)}, u32[]{:S(2)}) collective-permute-start(f32[72,56,38]{0,1,2:T(8,128)} %get-tuple-element.307), channel_id=1, source_target_pairs={{0,1},{1,2},{2,3},{3,4},{4,5},{5,6},{6,7},{7,0},{8,9},{9,10},{10,1... | collective-permute-start | bytes 1838600 | tf_op jit(solution)/shard_map/while/body/eval_jaxpr/ppermute | solution.py:36
  109.6 27.9 %collective-permute-start = (f32[72,56,39]{0,1,2:T(8,128)}, f32[72,56,39]{0,1,2:T(8,128)S(1)}, u32[]{:S(2)}, u32[]{:S(2)}) collective-permute-start(f32[72,56,39]{0,1,2:T(8,128)} %get-tuple-element.306), channel_id=1, source_target_pairs={{0,1},{1,2},{2,3},{3,4},{4,5},{5,6},{6,7},{7,0},{8,9},{9,10},{10,1... | collective-permute-start | bytes 1886984 | tf_op jit(solution)/shard_map/while/body/eval_jaxpr/ppermute | solution.py:35
  141.1 15.9 %collective-permute-start.1 = (f32[72,56,38]{0,1,2:T(8,128)}, f32[72,56,38]{0,1,2:T(8,128)S(1)}, u32[]{:S(2)}, u32[]{:S(2)}) collective-permute-start(f32[72,56,38]{0,1,2:T(8,128)} %get-tuple-element.307), channel_id=1, source_target_pairs={{0,1},{1,2},{2,3},{3,4},{4,5},{5,6},{6,7},{7,0},{8,9},{9,10},{10,1... | collective-permute-start | bytes 1838600 | tf_op jit(solution)/shard_map/while/body/eval_jaxpr/ppermute | solution.py:36
  141.1 27.9 %collective-permute-start = (f32[72,56,39]{0,1,2:T(8,128)}, f32[72,56,39]{0,1,2:T(8,128)S(1)}, u32[]{:S(2)}, u32[]{:S(2)}) collective-permute-start(f32[72,56,39]{0,1,2:T(8,128)} %get-tuple-element.306), channel_id=1, source_target_pairs={{0,1},{1,2},{2,3},{3,4},{4,5},{5,6},{6,7},{7,0},{8,9},{9,10},{10,1... | collective-permute-start | bytes 1886984 | tf_op jit(solution)/shard_map/while/body/eval_jaxpr/ppermute | solution.py:35
  172.7 15.9 %collective-permute-start.1 = (f32[72,56,38]{0,1,2:T(8,128)}, f32[72,56,38]{0,1,2:T(8,128)S(1)}, u32[]{:S(2)}, u32[]{:S(2)}) collective-permute-start(f32[72,56,38]{0,1,2:T(8,128)} %get-tuple-element.307), channel_id=1, source_target_pairs={{0,1},{1,2},{2,3},{3,4},{4,5},{5,6},{6,7},{7,0},{8,9},{9,10},{10,1... | collective-permute-start | bytes 1838600 | tf_op jit(solution)/shard_map/while/body/eval_jaxpr/ppermute | solution.py:36
  172.7 27.9 %collective-permute-start = (f32[72,56,39]{0,1,2:T(8,128)}, f32[72,56,39]{0,1,2:T(8,128)S(1)}, u32[]{:S(2)}, u32[]{:S(2)}) collective-permute-start(f32[72,56,39]{0,1,2:T(8,128)} %get-tuple-element.306), channel_id=1, source_target_pairs={{0,1},{1,2},{2,3},{3,4},{4,5},{5,6},{6,7},{7,0},{8,9},{9,10},{10,1... | collective-permute-start | bytes 1886984 | tf_op jit(solution)/shard_map/while/body/eval_jaxpr/ppermute | solution.py:35
  204.2 15.9 %collective-permute-start.1 = (f32[72,56,38]{0,1,2:T(8,128)}, f32[72,56,38]{0,1,2:T(8,128)S(1)}, u32[]{:S(2)}, u32[]{:S(2)}) collective-permute-start(f32[72,56,38]{0,1,2:T(8,128)} %get-tuple-element.307), channel_id=1, source_target_pairs={{0,1},{1,2},{2,3},{3,4},{4,5},{5,6},{6,7},{7,0},{8,9},{9,10},{10,1... | collective-permute-start | bytes 1838600 | tf_op jit(solution)/shard_map/while/body/eval_jaxpr/ppermute | solution.py:36
  204.2 27.9 %collective-permute-start = (f32[72,56,39]{0,1,2:T(8,128)}, f32[72,56,39]{0,1,2:T(8,128)S(1)}, u32[]{:S(2)}, u32[]{:S(2)}) collective-permute-start(f32[72,56,39]{0,1,2:T(8,128)} %get-tuple-element.306), channel_id=1, source_target_pairs={{0,1},{1,2},{2,3},{3,4},{4,5},{5,6},{6,7},{7,0},{8,9},{9,10},{10,1... | collective-permute-start | bytes 1886984 | tf_op jit(solution)/shard_map/while/body/eval_jaxpr/ppermute | solution.py:35
  235.8 15.9 %collective-permute-start.1 = (f32[72,56,38]{0,1,2:T(8,128)}, f32[72,56,38]{0,1,2:T(8,128)S(1)}, u32[]{:S(2)}, u32[]{:S(2)}) collective-permute-start(f32[72,56,38]{0,1,2:T(8,128)} %get-tuple-element.307), channel_id=1, source_target_pairs={{0,1},{1,2},{2,3},{3,4},{4,5},{5,6},{6,7},{7,0},{8,9},{9,10},{10,1... | collective-permute-start | bytes 1838600 | tf_op jit(solution)/shard_map/while/body/eval_jaxpr/ppermute | solution.py:36
  235.8 27.9 %collective-permute-start = (f32[72,56,39]{0,1,2:T(8,128)}, f32[72,56,39]{0,1,2:T(8,128)S(1)}, u32[]{:S(2)}, u32[]{:S(2)}) collective-permute-start(f32[72,56,39]{0,1,2:T(8,128)} %get-tuple-element.306), channel_id=1, source_target_pairs={{0,1},{1,2},{2,3},{3,4},{4,5},{5,6},{6,7},{7,0},{8,9},{9,10},{10,1... | collective-permute-start | bytes 1886984 | tf_op jit(solution)/shard_map/while/body/eval_jaxpr/ppermute | solution.py:35
  304.3 51.7 %copy-start.2 = (u32[128]{0:T(128)S(1)}, u32[128]{0:T(128)}, u32[]{:S(2)}) copy-start(u32[128]{0:T(128)} %constant.79) | copy-start | bytes 1540
  338.0 19.3 %collective-permute-start.4 = (f32[56,32]{0,1:T(8,128)S(1)}, f32[56,32]{0,1:T(8,128)S(1)}, u32[]{:S(2)}, u32[]{:S(2)}) collective-permute-start(f32[56,32]{0,1:T(8,128)S(1)} %get-tuple-element.239), channel_id=1, source_target_pairs={{0,8},{8,16},{16,24},{24,32},{32,40},{40,48},{48,56},{56,64},{64,7... | collective-permute-start | bytes 21512
  344.4 13.0 %collective-permute-start.5 = (f32[56,28]{0,1:T(8,128)S(1)}, f32[56,28]{0,1:T(8,128)S(1)}, u32[]{:S(2)}, u32[]{:S(2)}) collective-permute-start(f32[56,28]{0,1:T(8,128)S(1)} %slice.1), channel_id=1, source_target_pairs={{0,16},{8,24},{16,32},{24,40},{32,48},{40,56},{48,64},{56,72},{64,... | collective-permute-start | bytes 18824
  348.6 12.7 %collective-permute-start.2 = (f32[56,32]{0,1:T(8,128)S(1)}, f32[56,32]{0,1:T(8,128)S(1)}, u32[]{:S(2)}, u32[]{:S(2)}) collective-permute-start(f32[56,32]{0,1:T(8,128)S(1)} %get-tuple-element.238), channel_id=1, source_target_pairs={{0,8},{8,16},{16,24},{24,32},{32,40},{40,48},{48,56},{56,64},{64,7... | collective-permute-start | bytes 21512
  354.2 7.1 %collective-permute-start.3 = (f32[56,28]{0,1:T(8,128)S(1)}, f32[56,28]{0,1:T(8,128)S(1)}, u32[]{:S(2)}, u32[]{:S(2)}) collective-permute-start(f32[56,28]{0,1:T(8,128)S(1)} %slice), channel_id=1, source_target_pairs={{0,16},{8,24},{16,32},{24,40},{32,48},{40,56},{48,64},{56,72},{64,... | collective-permute-start | bytes 18824
where the time goes:
time: 364 us; the launch traced here: 362 us
  waiting for transfers between devices  161 us (44%)
  matrix products  81.6 us (22%)
  local copies, waits for them, and re-layouts  50.9 us (14%)
  blocking collectives  46.1 us (13%)
  starting transfers between devices  20.8 us (6%)
    ppermute x7, waiting for transfers between devices, pass_step(): visit_beta = lax.ppermute(visit_beta, 'orb', shift_pairs)  108 us
    ppermute x7, waiting for transfers between devices, pass_step(): visit_alpha = lax.ppermute(visit_alpha, 'orb', shift_pairs)  49.8 us
    unnamed x1, blocking collectives  33.5 us
    dot_general x16, matrix products, pair_product(): jnp.einsum('qmi,qni->mn', left, right, precision=TOP_PRECISION, preferred...  29 us
    unnamed x4, starting transfers between devices  18 us
    dot_general x1, matrix products, local_build(): jnp.einsum('qml,li->qmi', b_local, c_beta, precision=TOP_PRECISION, prefe...  15 us
    dot_general x1, matrix products, local_build(): jnp.einsum('qml,li->qmi', b_local, c_alpha, precision=TOP_PRECISION, pref...  14.8 us
    while x14, local copies, waits for them, and re-layouts  13.9 us
  transfers between devices with their start and end apart: 18, of which 15 were waited for; matrix products, arithmetic and copies ran while one was open for 10% of the time, Pallas kernels for 0%

commit v1 on v0

v1 whole, which is shorter than its diff:
```python
import functools

import jax
import jax.numpy as jnp
from jax import lax
from jax.experimental import pallas as pl
from jax.experimental.pallas import tpu as pltpu
from jax.sharding import PartitionSpec as P

TOP_PRECISION = lax.Precision.HIGHEST
F32 = jnp.float32
MESH = pl.DeviceIdType.MESH

NX, NC = 4, 2
NZ, NY = 4, 4
NORB = NX * NC
PACK = 3
LANES = 128
SLOT = 64
HALF = 32


def dot(a, b):
    return jnp.dot(a, b, precision=TOP_PRECISION, preferred_element_type=F32)


def kernel(dims, b_hbm, cw_ref, oa_ref, ob_ref,
           bbuf, tsend, trecv, tlhs, pbuf, gsend, grecv, gam, jblk, kbuf,
           xrecv, s1, r1, s2, r2, s3, r3,
           b_sem, ts_sem, tr_sem, gs_sem, gr_sem, xs_sem, xr_sem,
           s1_sem, r1_sem, s2_sem, r2_sem, s3_sem, r3_sem):
    ng, ml, nbas, na, nb = dims
    gpc = NC * ng
    aux = lax.axis_index("aux")
    me = lax.axis_index("orb")
    sysi = lax.axis_index("sys")
    xi, hi = me // NC, me % NC
    zi, yi = aux // NY, aux % NY
    partner = me + 1 - 2 * hi
    p_idx = jnp.where(hi == 0, zi, yi)
    s_idx = jnp.where(hi == 0, yi, zi)
    p_stride = jnp.where(hi == 0, NY, 1)
    s_stride = jnp.where(hi == 0, 1, NY)

    def first_peer(d):
        q = (p_idx + d) % NZ
        return q, (sysi, q * p_stride + s_idx * s_stride, me)

    def second_peer(d):
        q = (s_idx + d) % NZ
        return q, (sysi, p_idx * p_stride + q * s_stride, me)

    def orb_dev(o):
        return (sysi, aux, o)

    def b_copy(i, xp):
        return pltpu.make_async_copy(b_hbm.at[pl.ds(xp * gpc, gpc)],
                                     bbuf.at[pl.ds(xp * gpc, gpc)], b_sem.at[i])

    def chunk_chip(i):
        off = jnp.where(i == 0, 2, jnp.where(i == 1, 1, jnp.where(i == 2, 3, 0)))
        return (xi + off) % NX

    for i in range(NX):
        b_copy(i, chunk_chip(i)).start()

    barrier = pltpu.get_barrier_semaphore()
    for o in range(1, NORB):
        pl.semaphore_signal(barrier, inc=1, device_id=orb_dev((me + o) % NORB), device_id_type=MESH)
    for d in range(1, NZ):
        pl.semaphore_signal(barrier, inc=1, device_id=first_peer(d)[1], device_id_type=MESH)
        pl.semaphore_signal(barrier, inc=1, device_id=second_peer(d)[1], device_id_type=MESH)

    for sp in range(2):
        for s in range(NORB):
            trecv[sp, s * SLOT + ml:(s + 1) * SLOT, :] = jnp.zeros((SLOT - ml, ng * LANES), F32)

    def t_copy(sp, dest, src):
        return pltpu.make_async_remote_copy(
            src_ref=tsend.at[sp, dest], dst_ref=trecv.at[sp, pl.ds(pl.multiple_of(src * SLOT, SLOT), ml)],
            send_sem=ts_sem.at[sp, dest], recv_sem=tr_sem.at[sp, src],
            device_id=orb_dev(dest), device_id_type=MESH)

    row0 = pl.multiple_of(me * ml, 8)
    crow = sum(cw_ref[j, pl.ds(row0, ml), :] for j in range(PACK))

    def t_chunk(i, _):
        xp = chunk_chip(i)
        b_copy(i, xp).wait()
        acc = None
        for j in range(PACK):
            lhs = bbuf[pl.ds(xp * gpc, gpc), j].reshape(gpc * ml, nbas)
            part = dot(lhs, cw_ref[j])
            acc = part if acc is None else acc + part
        for hh in range(NC):
            for g in range(ng):
                k = hh * ng + g
                blk = acc[k * ml:(k + 1) * ml]
                tsend[0, NC * xp + hh, :, g * LANES:(g + 1) * LANES] = blk[:, :LANES]
                tsend[1, NC * xp + hh, :, g * LANES:(g + 1) * LANES] = blk[:, LANES:]
                pbuf[pl.ds(xp * gpc + k, 1), :] = jnp.sum(blk * crow, axis=0, keepdims=True)

        @pl.when(i == 0)
        def _():
            pl.semaphore_wait(barrier, NORB - 1 + 2 * (NZ - 1))

        for hh in range(NC):
            dest = NC * xp + hh

            @pl.when(dest != me)
            def _():
                t_copy(0, dest, me).start()
        return 0

    lax.fori_loop(0, NX, t_chunk, 0)

    ngrp = NX * gpc
    nrow = ngrp // 8
    lane_i = lax.broadcasted_iota(jnp.int32, (2 * LANES, LANES), 0)
    lane_o = lax.broadcasted_iota(jnp.int32, (2 * LANES, LANES), 1)
    seg = jnp.where(lane_i < LANES, lane_i // na, (lane_i - LANES) // nb)
    seg = jnp.where(seg < PACK, seg, -LANES)
    gpart = jnp.zeros((8, LANES), F32)
    for r in range(nrow):
        sel = jnp.where(seg + PACK * r == lane_o, 1.0, 0.0).astype(F32)
        gpart = gpart + dot(pbuf[8 * r:8 * r + 8, :], sel)
    gsend[...] = gpart

    def g_copy(dest, src):
        return pltpu.make_async_remote_copy(
            src_ref=gsend, dst_ref=grecv.at[src], send_sem=gs_sem.at[dest], recv_sem=gr_sem.at[src],
            device_id=orb_dev(dest), device_id_type=MESH)

    for o in range(1, NORB):
        g_copy((me + o) % NORB, me).start()
    grecv[me] = gpart
    for i in range(NX):
        xp = chunk_chip(i)
        for hh in range(NC):
            dest = NC * xp + hh
            if i < NX - 1:
                t_copy(1, dest, me).start()
            else:
                @pl.when(dest != me)
                def _():
                    t_copy(1, dest, me).start()
    for sp in range(2):
        trecv[sp, pl.ds(pl.multiple_of(me * SLOT, SLOT), ml), :] = tsend[sp, me]

    def x_copy(sp):
        keep = pl.multiple_of(16 - 16 * hi, 16)
        return pltpu.make_async_remote_copy(
            src_ref=kbuf.at[sp, :, pl.ds(keep, 16)], dst_ref=xrecv.at[sp],
            send_sem=xs_sem.at[sp], recv_sem=xr_sem.at[sp],
            device_id=orb_dev(partner), device_id_type=MESH)

    def p1_copy(sp, d):
        q, dev = first_peer(d)
        return pltpu.make_async_remote_copy(
            src_ref=s1.at[sp, q], dst_ref=r1.at[sp, d - 1], send_sem=s1_sem.at[sp, d - 1],
            recv_sem=r1_sem.at[sp, d - 1], device_id=dev, device_id_type=MESH)

    def p2_copy(sp, d):
        q, dev = second_peer(d)
        return pltpu.make_async_remote_copy(
            src_ref=s2.at[sp, q], dst_ref=r2.at[sp, d - 1], send_sem=s2_sem.at[sp, d - 1],
            recv_sem=r2_sem.at[sp, d - 1], device_id=dev, device_id_type=MESH)

    def p3_copy(sp, dest, src):
        return pltpu.make_async_remote_copy(
            src_ref=s3.at[sp, dest // NC], dst_ref=r3.at[sp, src], send_sem=s3_sem.at[sp, dest],
            recv_sem=r3_sem.at[sp, src], device_id=orb_dev(dest), device_id_type=MESH)

    def exchange(sp):
        for o in range(1, NORB):
            src = (me + o) % NORB
            t_copy(sp, src, src).wait_recv()
        for s in range(NORB):
            base = s * SLOT
            tlhs[base:base + HALF, :] = trecv[sp, base:base + HALF, :]
            tlhs[base + HALF:base + SLOT, :] = trecv[sp, base + ml // 2:base + ml // 2 + HALF, :]
        nt = (((1,), (1,)), ((), ()))

        def rows(c, _):
            r0 = pl.multiple_of(c * 256, 256)
            prod = lax.dot_general(tlhs[pl.ds(r0, 256), :], trecv[sp], nt,
                                   precision=TOP_PRECISION, preferred_element_type=F32)
            kbuf[sp, pl.ds(c * 8, 8)] = (-prod).reshape(8, HALF, NORB * SLOT)
            return 0

        lax.fori_loop(0, 2, rows, 0)

    def coulomb():
        for o in range(1, NORB):
            src = (me + o) % NORB
            g_copy(src, src).wait_recv()
        gsum = grecv[0]
        for s in range(1, NORB):
            gsum = gsum + grecv[s]
        for r in range(nrow):
            for j in range(PACK):
                c = PACK * r + j
                gam[c * 8:c * 8 + 8, :] = jnp.broadcast_to(gsum[:, c:c + 1], (8, LANES))

        def add(g, acc):
            r, row = g // 8, g % 8
            for j in range(PACK):
                w = gam[pl.ds((PACK * r + j) * 8 + row, 1), :][:, :1]
                acc = acc + bbuf[g, j] * w
            return acc

        jmat = lax.fori_loop(0, ngrp, add, jnp.zeros((ml, nbas), F32))
        col = lax.broadcasted_iota(jnp.int32, (nbas, NORB * SLOT), 0)
        lane = lax.broadcasted_iota(jnp.int32, (nbas, NORB * SLOT), 1)
        spread = jnp.where((col // ml) * SLOT + col % ml == lane, 1.0, 0.0).astype(F32)
        jblk[...] = dot(jmat, spread)

    def add_coulomb(sp):
        half = ml // 2
        kbuf[sp, 2 * me, 0:half, :] = kbuf[sp, 2 * me, 0:half, :] + jblk[0:half, :]
        kbuf[sp, 2 * me + 1, 0:half, :] = kbuf[sp, 2 * me + 1, 0:half, :] + jblk[half:ml, :]
        x_copy(sp).start()

    def stage1(sp):
        x_copy(sp).wait_recv()
        mine = pl.multiple_of(16 * hi, 16)
        for p in range(NZ):
            for s in range(NY):
                slot = jnp.where(hi == 0, NY * p + s, NY * s + p)
                s1[sp, p, s] = kbuf[sp, slot, pl.ds(mine, 16), :] + xrecv[sp, slot]
        for d in (2, 1, 3):
            p1_copy(sp, d).start()

    def stage2(sp):
        for d in (1, 3, 2):
            p1_copy(sp, d).wait_recv()
        s2[sp] = ((s1[sp, p_idx] + r1[sp, 0]) + r1[sp, 1]) + r1[sp, 2]
        for d in (2, 1, 3):
            p2_copy(sp, d).start()

    def stage3(sp):
        for d in (1, 3, 2):
            p2_copy(sp, d).wait_recv()
        tot = ((s2[sp, s_idx] + r2[sp, 0]) + r2[sp, 1]) + r2[sp, 2]
        for x in range(NX):
            s3[sp, x] = tot[:, x * LANES:(x + 1) * LANES]
        for o in range(1, NORB):
            p3_copy(sp, (me + o) % NORB, me).start()
        r3[sp, me] = s3[sp, xi]

    def finish(sp, o_ref):
        for o in range(1, NORB):
            src = (me + o) % NORB
            p3_copy(sp, src, src).wait_recv()
        for h in range(NC):
            tot = r3[sp, h]
            for x in range(1, NX):
                tot = tot + r3[sp, NC * x + h]
            o_ref[16 * h:16 * h + 16, :] = tot

    exchange(0)
    coulomb()
    add_coulomb(0)
    stage1(0)
    exchange(1)
    add_coulomb(1)
    stage2(0)
    stage1(1)
    stage3(0)
    stage2(1)
    stage3(1)
    finish(0, oa_ref)
    finish(1, ob_ref)

    for sp in range(2):
        for o in range(1, NORB):
            dest = (me + o) % NORB
            t_copy(sp, dest, me).wait_send()
            p3_copy(sp, dest, me).wait_send()
        x_copy(sp).wait_send()
        for d in range(1, NZ):
            p1_copy(sp, d).wait_send()
            p2_copy(sp, d).wait_send()
    for o in range(1, NORB):
        g_copy((me + o) % NORB, me).wait_send()


def solution(mesh):
    def local_build(b_local, c_alpha, c_beta):
        q_loc, ml, nbas = b_local.shape
        na, nb = c_alpha.shape[1], c_beta.shape[1]
        ng = q_loc // (PACK * NORB)
        packed = []
        for j in range(PACK):
            packed.append(jnp.concatenate([
                jnp.pad(c_alpha, ((0, 0), (na * j, LANES - na * (j + 1)))),
                jnp.pad(c_beta, ((0, 0), (nb * j, LANES - nb * (j + 1))))], axis=1))
        cw = jnp.stack(packed)
        b4 = b_local.reshape(q_loc // PACK, PACK, ml, nbas)
        lanes = ng * LANES
        width = NORB * SLOT
        dma = pltpu.SemaphoreType.DMA
        out = pl.pallas_call(
            functools.partial(kernel, (ng, ml, nbas, na, nb)),
            out_shape=[jax.ShapeDtypeStruct((HALF, LANES), F32)] * 2,
            in_specs=[pl.BlockSpec(memory_space=pl.ANY), pl.BlockSpec(memory_space=pltpu.VMEM)],
            out_specs=[pl.BlockSpec(memory_space=pltpu.VMEM)] * 2,
            scratch_shapes=[
                pltpu.VMEM(b4.shape, F32),
                pltpu.VMEM((2, NORB, ml, lanes), F32),
                pltpu.VMEM((2, width, lanes), F32),
                pltpu.VMEM((width, lanes), F32),
                pltpu.VMEM((q_loc // PACK, 2 * LANES), F32),
                pltpu.VMEM((8, LANES), F32),
                pltpu.VMEM((NORB, 8, LANES), F32),
                pltpu.VMEM((q_loc, LANES), F32),
                pltpu.VMEM((ml, width), F32),
                pltpu.VMEM((2, NZ * NY, HALF, width), F32),
                pltpu.VMEM((2, NZ * NY, HALF // 2, width), F32),
                pltpu.VMEM((2, NZ, NY, HALF // 2, width), F32),
                pltpu.VMEM((2, NZ - 1, NY, HALF // 2, width), F32),
                pltpu.VMEM((2, NY, HALF // 2, width), F32),
                pltpu.VMEM((2, NZ - 1, HALF // 2, width), F32),
                pltpu.VMEM((2, NX, HALF // 2, LANES), F32),
                pltpu.VMEM((2, NORB, HALF // 2, LANES), F32),
                dma((NX,)), dma((2, NORB)), dma((2, NORB)), dma((NORB,)), dma((NORB,)),
                dma((2,)), dma((2,)),
                dma((2, NZ - 1)), dma((2, NZ - 1)), dma((2, NZ - 1)), dma((2, NZ - 1)),
                dma((2, NORB)), dma((2, NORB)),
            ],
            compiler_params=pltpu.CompilerParams(
                collective_id=0, has_side_effects=True, vmem_limit_bytes=60 * 1024 * 1024),
        )(b4, cw)
        core = lax.axis_index("orb") % NC
        n_aux_cols = nbas // (NZ * NY)

        def place(block):
            half = jnp.where(core == 0, block[:, :SLOT], block[:, SLOT:])
            return half[:n_aux_cols, :ml].T

        return place(out[0]), place(out[1])

    spec_b = P(('sys', 'aux'), 'orb', None)
    spec_c = P('sys', None)
    spec_g = P(('sys', 'orb'), 'aux')
    return jax.shard_map(local_build, mesh=mesh, in_specs=(spec_b, spec_c, spec_c), out_specs=(spec_g, spec_g), check_vma=False)
```

time: 364 us -> 54.8 us (0.15)
  the two profiles are of different devices: /device:TPU:88 before, /device:TPU:1 now
where the time goes in v1:
time: 54.8 us; the launch traced here: 54.5 us
  Pallas kernels  48.2 us (88%)
  local copies, waits for them, and re-layouts  2.91 us (5%)
  other arithmetic  2.72 us (5%)
  between operations  0.65 us (1%)
    pallas_call x1, Pallas kernels, local_build(): pl.pallas_call(functools.partial(kernel, (ng, ml, nbas, na, nb)), out_sha...  48.2 us
    unnamed x2, local copies, waits for them, and re-layouts  2.04 us
    another operation x2, other arithmetic, local_build(): cw = jnp.stack(packed)  1.5 us
    transpose x2, other arithmetic, place(): return half[:n_aux_cols, :ml].T  1.22 us

profile of v1, /device:TPU:1, one launch (start us, length us, event | category | flops | bytes accessed | tf_op | source)
XLA Modules:
  0.0 54.5 jit_solution(10824010754958223248)
XLA Ops:
  0.6 1.0 %copy.6 = f32[448,38]{1,0:T(8,128)S(1)} copy(f32[448,38]{0,1:T(8,128)} %param.5) | data formatting | bytes 136192 | tf_op args[2]
  1.6 1.0 %copy.5 = f32[448,39]{1,0:T(8,128)S(1)} copy(f32[448,39]{0,1:T(8,128)} %param.4) | data formatting | bytes 139776 | tf_op args[1]
  2.7 0.3 fusion.2
  3.0 1.2 %pad_maximum_fusion.cw_ref = f32[3,448,256]{2,1,0:T(8,128)} fusion(f32[1,448,256]{2,1,0:T(8,128)S(1)} %get-tuple-element.7, f32[1,448,256]{2,1,0:T(8,128)S(1)} %get-tuple-element.8, f32[1,448,256]{2,1,0:T(8,128)S(1)} %get-tuple-element.6), kind=kLoop, calls=%fused_computation | loop fusion | flops 688128 | bytes 2752512 | tf_op jit(solution)/shard_map/stack | solution.py:298
  4.2 48.2 %shard_map.50 = (f32[32,128]{1,0:T(8,128)}, f32[32,128]{1,0:T(8,128)}) custom-call(f32[24,3,56,448]{3,2,1,0:T(8,128)} %bitcast.11, f32[3,448,256]{2,1,0:T(8,128)} %pad_maximum_fusion.cw_ref), custom_call_target="tpu_custom_call" | custom-call | tf_op jit(solution)/shard_map/pallas_call | solution.py:303
  52.4 0.9 %fusion.5 = (f32[32,64]{1,0:T(8,128)S(1)}, f32[32,64]{1,0:T(8,128)S(1)}, f32[32,64]{1,0:T(8,128)S(1)}, f32[32,64]{1,0:T(8,128)S(1)}) fusion(f32[32,128]{1,0:T(8,128)} %get-tuple-element.5, f32[32,128]{1,0:T(8,128)} %get-tuple-element.4), kind=kLoop, calls=%fused_computation.13 | loop fusion | bytes 65536 | tf_op jit(solution)/shard_map/slice | solution.py:338
  53.3 0.6 %fusion.4 = f32[56,28]{0,1:T(8,128)} fusion(f32[32,64]{1,0:T(8,128)S(1)} %get-tuple-element.13, f32[32,64]{1,0:T(8,128)S(1)} %get-tuple-element.14, pred[]{:T(512)S(6)} %eq.6), kind=kLoop, calls=%fused_computation.12 | loop fusion | flops 1568 | bytes 18817 | tf_op jit(solution)/shard_map/transpose | solution.py:339
  53.9 0.6 %fusion.3 = f32[56,28]{0,1:T(8,128)} fusion(f32[32,64]{1,0:T(8,128)S(1)} %get-tuple-element.10, f32[32,64]{1,0:T(8,128)S(1)} %get-tuple-element.9, pred[]{:T(512)S(6)} %eq.6), kind=kLoop, calls=%fused_computation.10 | loop fusion | flops 1568 | bytes 18817 | tf_op jit(solution)/shard_map/transpose | solution.py:339

commit v2 on v1

v2 whole, which is shorter than its diff:
```python
import functools

import jax
import jax.numpy as jnp
from jax import lax
from jax.experimental import pallas as pl
from jax.experimental.pallas import tpu as pltpu
from jax.sharding import PartitionSpec as P

TOP_PRECISION = lax.Precision.HIGHEST
F32 = jnp.float32
MESH = pl.DeviceIdType.MESH

NX, NC = 4, 2
NZ, NY = 4, 4
NORB = NX * NC
PACK = 3
LANES = 128
SLOT = 64
HALF = 32
WIDE = NORB * SLOT // NC
NT = (((1,), (1,)), ((), ()))


def dot(a, b):
    return jnp.dot(a, b, precision=TOP_PRECISION, preferred_element_type=F32)


def dot_nt(a, b):
    return lax.dot_general(a, b, NT, precision=TOP_PRECISION, preferred_element_type=F32)


def iota(shape, dim):
    return lax.broadcasted_iota(jnp.int32, shape, dim)


def kernel(dims, b_hbm, ca_ref, cb_ref, oa_ref, ob_ref,
           bbuf, cwt, tsend, rel, trecv, tlhs, pbuf, gsend, grecv, gam, jown, jother, jfull,
           kbuf, r1, s2, r2, s3, r3,
           b_sem, ts_sem, tr_sem, rr_sem, rs_sem, ps_sem, pr_sem, gs_sem, gr_sem, j_sem,
           s1_sem, r1_sem, s2_sem, r2_sem, s3_sem, r3_sem):
    ng, ml, nbas, na, nb = dims
    gpc = NC * ng
    lanes = ng * LANES
    cols = nbas // (NZ * NY)
    aux = lax.axis_index("aux")
    me = lax.axis_index("orb")
    sysi = lax.axis_index("sys")
    xi, hi = me // NC, me % NC
    zi, yi = aux // NY, aux % NY
    partner = me + 1 - 2 * hi
    step = 1 + 2 * hi
    p_idx = jnp.where(hi == 0, zi, yi)
    s_idx = jnp.where(hi == 0, yi, zi)
    p_stride = jnp.where(hi == 0, NY, 1)
    s_stride = jnp.where(hi == 0, 1, NY)

    def first_peer(d):
        q = (p_idx + d) % NZ
        return q, (sysi, q * p_stride + s_idx * s_stride, me)

    def second_peer(d):
        q = (s_idx + d) % NZ
        return q, (sysi, p_idx * p_stride + q * s_stride, me)

    def orb_dev(o):
        return (sysi, aux, o)

    def remote(src, dst, send, recv, dev):
        return pltpu.make_async_remote_copy(src_ref=src, dst_ref=dst, send_sem=send, recv_sem=recv,
                                            device_id=dev, device_id_type=MESH)

    def b_copy(i, xp):
        return pltpu.make_async_copy(b_hbm.at[pl.ds(xp * gpc, gpc)],
                                     bbuf.at[pl.ds(xp * gpc, gpc)], b_sem.at[i])

    def chunk_chip(i):
        near = jnp.where(i == 1, step, NX - step)
        off = jnp.where(i == 0, 2, jnp.where(i == NX - 1, 0, near))
        return (xi + off) % NX

    for i in range(NX):
        b_copy(i, chunk_chip(i)).start()

    barrier = pltpu.get_barrier_semaphore()
    for o in range(1, NORB):
        pl.semaphore_signal(barrier, inc=1, device_id=orb_dev((me + o) % NORB), device_id_type=MESH)
    for d in range(1, NZ):
        pl.semaphore_signal(barrier, inc=1, device_id=first_peer(d)[1], device_id_type=MESH)
        pl.semaphore_signal(barrier, inc=1, device_id=second_peer(d)[1], device_id_type=MESH)

    for j in range(PACK):
        cwt[j] = jnp.zeros((2 * LANES, nbas), F32)
        cwt[j, na * j:na * (j + 1), :] = ca_ref[...]
        cwt[j, LANES + nb * j:LANES + nb * (j + 1), :] = cb_ref[...]
    for sp in range(2):
        for s in range(NORB):
            trecv[sp, s * SLOT + ml:(s + 1) * SLOT, :] = jnp.zeros((SLOT - ml, NC * lanes), F32)
        for s in range(NY):
            s2[sp, s, HALF - 8:HALF, :] = jnp.zeros((8, WIDE), F32)
    rowsel = jnp.where(iota((ml, nbas), 1) == me * ml + iota((ml, nbas), 0), 1.0, 0.0).astype(F32)
    crow = dot_nt(rowsel, cwt[0] + cwt[1] + cwt[2])

    def rows_of(src):
        return pl.ds(pl.multiple_of(src * SLOT, SLOT), ml)

    def t_copy(sp, dest, src):
        return remote(tsend.at[sp, dest], trecv.at[sp, rows_of(src), pl.ds(0, lanes)],
                      ts_sem.at[sp, dest], tr_sem.at[sp, src], orb_dev(dest))

    def relay_in(sp, hh):
        dest = NC * ((xi + 2) % NX) + hh
        return remote(tsend.at[sp, dest], rel.at[sp, hh], ts_sem.at[sp, dest], rr_sem.at[sp, hh],
                      orb_dev(NC * ((xi + step) % NX) + hi))

    def relay_out(sp, hh):
        src = NC * ((xi + NX - step) % NX) + hi
        return remote(rel.at[sp, hh], trecv.at[sp, rows_of(src), pl.ds(0, lanes)],
                      rs_sem.at[sp, hh], tr_sem.at[sp, src], orb_dev(NC * ((xi + step) % NX) + hh))

    def share(sp, src):
        return remote(trecv.at[sp, rows_of(src), pl.ds(0, lanes)],
                      trecv.at[sp, rows_of(src), pl.ds(lanes, lanes)],
                      ps_sem.at[sp, src], pr_sem.at[sp, src], orb_dev(partner))

    def share_own(sp):
        return remote(tsend.at[sp, me], trecv.at[sp, rows_of(me), pl.ds(lanes, lanes)],
                      ps_sem.at[sp, me], pr_sem.at[sp, me], orb_dev(partner))

    def t_chunk(i, _):
        xp = chunk_chip(i)
        b_copy(i, xp).wait()
        acc = None
        for j in range(PACK):
            lhs = bbuf[pl.ds(xp * gpc, gpc), j].reshape(gpc * ml, nbas)
            part = dot_nt(lhs, cwt[j])
            acc = part if acc is None else acc + part
        for hh in range(NC):
            for g in range(ng):
                k = hh * ng + g
                blk = acc[k * ml:(k + 1) * ml]
                tsend[0, NC * xp + hh, :, g * LANES:(g + 1) * LANES] = blk[:, :LANES]
                tsend[1, NC * xp + hh, :, g * LANES:(g + 1) * LANES] = blk[:, LANES:]
                pbuf[pl.ds(xp * gpc + k, 1), :] = jnp.sum(blk * crow, axis=0, keepdims=True)

        @pl.when(i == 0)
        def _():
            pl.semaphore_wait(barrier, NORB - 1 + 2 * (NZ - 1))
            for sp in range(2):
                for hh in range(NC):
                    relay_in(sp, hh).start()

        @pl.when((i == 1) | (i == 2))
        def _():
            for hh in range(NC):
                t_copy(0, NC * xp + hh, me).start()

        @pl.when(i == NX - 1)
        def _():
            t_copy(0, partner, me).start()
            share_own(0).start()
        return 0

    lax.fori_loop(0, NX, t_chunk, 0)

    for hh in range(NC):
        relay_in(0, hh).wait_recv()
        relay_out(0, hh).start()

    ngrp = NX * gpc
    nrow = ngrp // 8
    lane_i = iota((2 * LANES, LANES), 0)
    lane_o = iota((2 * LANES, LANES), 1)
    seg = jnp.where(lane_i < LANES, lane_i // na, (lane_i - LANES) // nb)
    seg = jnp.where(seg < PACK, seg, -LANES)
    gpart = jnp.zeros((8, LANES), F32)
    for r in range(nrow):
        sel = jnp.where(seg + PACK * r == lane_o, 1.0, 0.0).astype(F32)
        gpart = gpart + dot(pbuf[8 * r:8 * r + 8, :], sel)
    gsend[...] = gpart

    def g_copy(dest, src):
        return remote(gsend, grecv.at[src], gs_sem.at[dest], gr_sem.at[src], orb_dev(dest))

    for o in range(1, NORB):
        g_copy((me + o) % NORB, me).start()
    grecv[me] = gpart
    near = [NC * chunk_chip(i) + hh for i in (1, 2) for hh in range(NC)]
    far = [NC * ((xi + 2) % NX) + hh for hh in range(NC)]
    for dest in near:
        t_copy(1, dest, me).start()
    t_copy(1, partner, me).start()
    share_own(1).start()
    for sp in range(2):
        trecv[sp, rows_of(me), 0:lanes] = tsend[sp, me]
        trecv[sp, rows_of(me), lanes:2 * lanes] = tsend[sp, partner]

    def pass_on(sp, sources):
        for src in sources:
            t_copy(sp, src, src).wait_recv()
            share(sp, src).start()

    def j_copy():
        return remote(jown.at[1 - hi], jother, j_sem.at[0], j_sem.at[1], orb_dev(partner))

    def p1_copy(sp, d):
        q, dev = first_peer(d)
        return remote(kbuf.at[sp, q], r1.at[sp, d - 1], s1_sem.at[sp, d - 1], r1_sem.at[sp, d - 1], dev)

    def p2_copy(sp, d):
        q, dev = second_peer(d)
        return remote(s2.at[sp, q], r2.at[sp, d - 1], s2_sem.at[sp, d - 1], r2_sem.at[sp, d - 1], dev)

    def p3_copy(sp, k):
        return remote(s3.at[sp, k // NC], r3.at[sp, xi], s3_sem.at[sp, k], r3_sem.at[sp, xi],
                      orb_dev(NX * hi + k))

    def p3_wait(sp, x):
        return remote(s3.at[sp, 0], r3.at[sp, x], s3_sem.at[sp, 0], r3_sem.at[sp, x],
                      orb_dev(NC * x + xi // NC))

    def coulomb():
        for o in range(1, NORB):
            src = (me + o) % NORB
            g_copy(src, src).wait_recv()
        gsum = grecv[0]
        for s in range(1, NORB):
            gsum = gsum + grecv[s]
        for r in range(nrow):
            for j in range(PACK):
                c = PACK * r + j
                gam[c * 8:c * 8 + 8, :] = jnp.broadcast_to(gsum[:, c:c + 1], (8, LANES))

        def add(g, acc):
            r, row = g // 8, g % 8
            for j in range(PACK):
                w = gam[pl.ds((PACK * r + j) * 8 + row, 1), :][:, :1]
                acc = acc + bbuf[g, j] * w
            return acc

        jmat = lax.fori_loop(0, ngrp, add, jnp.zeros((ml, nbas), F32))
        col = iota((nbas, NORB * SLOT), 0)
        spread = jnp.where((col // ml) * SLOT + col % ml == iota((nbas, NORB * SLOT), 1), 1.0, 0.0).astype(F32)
        wide = dot(jmat, spread)
        for h in range(NC):
            jown[h] = wide[:, h * WIDE:(h + 1) * WIDE]
        j_copy().start()
        row, r = iota((nbas, ml), 0), iota((nbas, ml), 1)
        pos = row // cols
        nat = jnp.where(hi == 0, pos, (pos % NZ) * NY + pos // NZ) * cols + row % cols
        own = jnp.where(nat == me * ml + r, 1.0, 0.0).astype(F32)
        other = jnp.where(nat == partner * ml + r, 1.0, 0.0).astype(F32)
        mine = dot(own, jown[hi])
        j_copy().wait_recv()
        jfull[...] = (mine + dot(other, jother[...])).reshape(NZ, NY * cols, WIDE)

    def exchange(sp):
        for o in range(1, NORB):
            share(sp, (me + o) % NORB).wait_recv()
        for h in range(NC):
            @pl.when(hi == h)
            def _():
                for a in range(NZ * NY):
                    at = a if h == 0 else (a % NY) * NZ + a // NY
                    base = (a // 2) * SLOT + (a % 2) * cols
                    tlhs[at * cols:(at + 1) * cols, :] = trecv[sp, base:base + cols, :]
        rhs = pl.ds(pl.multiple_of(WIDE * hi, WIDE), WIDE)

        def rows(c, _):
            r0 = pl.multiple_of(c * (2 * NY * cols), 8)
            prod = dot_nt(tlhs[pl.ds(r0, 2 * NY * cols), :], trecv[sp, rhs, :])
            kbuf[sp, pl.ds(2 * c, 2)] = jfull[pl.ds(2 * c, 2)] - prod.reshape(2, NY * cols, WIDE)
            return 0

        lax.fori_loop(0, NZ // 2, rows, 0)
        for d in (2, 1, 3):
            p1_copy(sp, d).start()

    def stage2(sp):
        for d in (1, 3, 2):
            p1_copy(sp, d).wait_recv()
        tot = ((kbuf[sp, p_idx] + r1[sp, 0]) + r1[sp, 1]) + r1[sp, 2]
        for s in range(NY):
            s2[sp, s, 0:cols, :] = tot[s * cols:(s + 1) * cols]
        for d in (2, 1, 3):
            p2_copy(sp, d).start()

    def stage3(sp):
        for d in (1, 3, 2):
            p2_copy(sp, d).wait_recv()
        tot = ((s2[sp, s_idx] + r2[sp, 0]) + r2[sp, 1]) + r2[sp, 2]
        for x in range(NX // NC):
            s3[sp, x] = tot[:, x * LANES:(x + 1) * LANES]
        for k in range(NX):
            @pl.when(NX * hi + k != me)
            def _():
                p3_copy(sp, k).start()

            @pl.when(NX * hi + k == me)
            def _():
                r3[sp, xi] = s3[sp, k // NC]

    def finish(sp, o_ref):
        for x in range(NX):
            @pl.when(NC * x + xi // NC != me)
            def _():
                p3_wait(sp, x).wait_recv()
        tot = ((r3[sp, 0] + r3[sp, 1]) + r3[sp, 2]) + r3[sp, 3]
        half = jnp.where(hi == 0, tot[:, :SLOT], tot[:, SLOT:])
        o_ref[...] = half[:cols, :ml]

    pass_on(0, near)
    for hh in range(NC):
        relay_in(1, hh).wait_recv()
        relay_out(1, hh).start()
    pass_on(0, far)
    t_copy(0, partner, partner).wait_recv()
    coulomb()
    exchange(0)
    pass_on(1, near)
    pass_on(1, far)
    t_copy(1, partner, partner).wait_recv()
    exchange(1)
    stage2(0)
    stage3(0)
    stage2(1)
    stage3(1)
    finish(0, oa_ref)
    finish(1, ob_ref)

    for sp in range(2):
        for dest in near + [partner]:
            t_copy(sp, dest, me).wait_send()
        for hh in range(NC):
            relay_in(sp, hh).wait_send()
            relay_out(sp, hh).wait_send()
        for src in near + far:
            share(sp, src).wait_send()
        share_own(sp).wait_send()
        for d in range(1, NZ):
            p1_copy(sp, d).wait_send()
            p2_copy(sp, d).wait_send()
        for k in range(NX):
            @pl.when(NX * hi + k != me)
            def _():
                p3_copy(sp, k).wait_send()
    for o in range(1, NORB):
        g_copy((me + o) % NORB, me).wait_send()
    j_copy().wait_send()


def solution(mesh):
    def local_build(b_local, c_alpha, c_beta):
        q_loc, ml, nbas = b_local.shape
        na, nb = c_alpha.shape[1], c_beta.shape[1]
        ng = q_loc // (PACK * NORB)
        b4 = b_local.reshape(q_loc // PACK, PACK, ml, nbas)
        lanes = ng * LANES
        width = NORB * SLOT
        cols = nbas // (NZ * NY)
        dma = pltpu.SemaphoreType.DMA
        vmem = pl.BlockSpec(memory_space=pltpu.VMEM)
        out = pl.pallas_call(
            functools.partial(kernel, (ng, ml, nbas, na, nb)),
            out_shape=[jax.ShapeDtypeStruct((cols, ml), F32)] * 2,
            in_specs=[pl.BlockSpec(memory_space=pl.ANY), vmem, vmem],
            out_specs=[vmem] * 2,
            scratch_shapes=[
                pltpu.VMEM(b4.shape, F32),
                pltpu.VMEM((PACK, 2 * LANES, nbas), F32),
                pltpu.VMEM((2, NORB, ml, lanes), F32),
                pltpu.VMEM((2, NC, ml, lanes), F32),
                pltpu.VMEM((2, width, NC * lanes), F32),
                pltpu.VMEM((nbas, NC * lanes), F32),
                pltpu.VMEM((q_loc // PACK, 2 * LANES), F32),
                pltpu.VMEM((8, LANES), F32),
                pltpu.VMEM((NORB, 8, LANES), F32),
                pltpu.VMEM((q_loc, LANES), F32),
                pltpu.VMEM((NC, ml, WIDE), F32),
                pltpu.VMEM((ml, WIDE), F32),
                pltpu.VMEM((NZ, NY * cols, WIDE), F32),
                pltpu.VMEM((2, NZ, NY * cols, WIDE), F32),
                pltpu.VMEM((2, NZ - 1, NY * cols, WIDE), F32),
                pltpu.VMEM((2, NY, HALF, WIDE), F32),
                pltpu.VMEM((2, NZ - 1, HALF, WIDE), F32),
                pltpu.VMEM((2, NX // NC, HALF, LANES), F32),
                pltpu.VMEM((2, NX, HALF, LANES), F32),
                dma((NX,)), dma((2, NORB)), dma((2, NORB)), dma((2, NC)), dma((2, NC)),
                dma((2, NORB)), dma((2, NORB)), dma((NORB,)), dma((NORB,)), dma((2,)),
                dma((2, NZ - 1)), dma((2, NZ - 1)), dma((2, NZ - 1)), dma((2, NZ - 1)),
                dma((2, NX)), dma((2, NX)),
            ],
            compiler_params=pltpu.CompilerParams(
                collective_id=0, has_side_effects=True, vmem_limit_bytes=60 * 1024 * 1024),
        )(b4, c_alpha.T, c_beta.T)
        return out[0].T, out[1].T

    spec_b = P(('sys', 'aux'), 'orb', None)
    spec_c = P('sys', None)
    spec_g = P(('sys', 'orb'), 'aux')
    return jax.shard_map(local_build, mesh=mesh, in_specs=(spec_b, spec_c, spec_c), out_specs=(spec_g, spec_g), check_vma=False)
```

time: 54.8 us -> 53.8 us (0.982)
  other arithmetic: 2.72 us -> 0 us
  Pallas kernels: 48.2 us -> 50.2 us
    pallas_call x1, Pallas kernels: 48.2 us -> 50.2 us  [local_build(): pl.pallas_call(functools.partial(kernel, (ng, ml, nbas, na, nb)), out_sha...]
    another operation x2 -> x0, other arithmetic: 1.5 us -> none  [local_build(): cw = jnp.stack(packed)]
    transpose x2 -> x0, other arithmetic: 1.22 us -> none  [place(): return half[:n_aux_cols, :ml].T]
    slice x1 -> x0, local copies, waits for them, and re-layouts: 0.87 us -> none  [place(): half = jnp.where(core == 0, block[:, :SLOT], block[:, SLOT:])]
    unnamed x2, local copies, waits for them, and re-layouts: 2.04 us -> 2.65 us
where the time goes in v2:
time: 53.8 us; the launch traced here: 53.5 us
  Pallas kernels  50.2 us (93%)
  local copies, waits for them, and re-layouts  2.65 us (5%)
  between operations  0.64 us (1%)
    pallas_call x1, Pallas kernels, local_build(): pl.pallas_call(functools.partial(kernel, (ng, ml, nbas, na, nb)), out_sha...  50.2 us
    unnamed x2, local copies, waits for them, and re-layouts  2.65 us

profile of v2, /device:TPU:1, one launch (start us, length us, event | category | flops | bytes accessed | tf_op | source)
XLA Modules:
  0.0 53.5 jit_solution(16286549286443503379)
XLA Ops:
  0.6 50.2 %shard_map.50 = (f32[28,56]{1,0:T(8,128)}, f32[28,56]{1,0:T(8,128)}) custom-call(f32[24,3,56,448]{3,2,1,0:T(8,128)} %bitcast.5, f32[39,448]{1,0:T(8,128)} %bitcast.6, f32[38,448]{1,0:T(8,128)} %bitcast.7), custom_call_target="tpu_custom_call" | custom-call | tf_op jit(solution)/shard_map/pallas_call | solution.py:363
  50.8 1.3 %copy.7 = f32[56,28]{0,1:T(8,128)} copy(f32[56,28]{0,1:T(8,128)} %bitcast.9) | data formatting | bytes 12544
  52.1 1.3 %copy.8 = f32[56,28]{0,1:T(8,128)} copy(f32[56,28]{0,1:T(8,128)} %bitcast.8) | data formatting | bytes 12544

commit v3 on v2

--- a/solution.py
+++ b/solution.py
@@ -14,6 +14,7 @@
 NX, NC = 4, 2
 NZ, NY = 4, 4
 NORB = NX * NC
+NAUX = NZ * NY
 PACK = 3
 LANES = 128
 SLOT = 64
@@ -35,9 +36,9 @@
 
 
 def kernel(dims, b_hbm, ca_ref, cb_ref, oa_ref, ob_ref,
-           bbuf, cwt, tsend, rel, trecv, tlhs, pbuf, gsend, grecv, gam, jown, jother, jfull,
+           bbuf, cwt, tsend, trecv, tlhs, pbuf, gsend, grecv, gam, jpad, jsend, jrecv,
            kbuf, r1, s2, r2, s3, r3,
-           b_sem, ts_sem, tr_sem, rr_sem, rs_sem, ps_sem, pr_sem, gs_sem, gr_sem, j_sem,
+           b_sem, ts_sem, tr_sem, ps_sem, pr_sem, gs_sem, gr_sem, js_sem, jr_sem,
            s1_sem, r1_sem, s2_sem, r2_sem, s3_sem, r3_sem):
     ng, ml, nbas, na, nb = dims
     gpc = NC * ng
@@ -75,8 +76,8 @@
                                      bbuf.at[pl.ds(xp * gpc, gpc)], b_sem.at[i])
 
     def chunk_chip(i):
-        near = jnp.where(i == 1, step, NX - step)
-        off = jnp.where(i == 0, 2, jnp.where(i == NX - 1, 0, near))
+        near = jnp.where(i == 2, step, NX - step)
+        off = jnp.where(i == 0, 2, jnp.where(i == 1, 0, near))
         return (xi + off) % NX
 
     for i in range(NX):
@@ -85,9 +86,8 @@
     barrier = pltpu.get_barrier_semaphore()
     for o in range(1, NORB):
         pl.semaphore_signal(barrier, inc=1, device_id=orb_dev((me + o) % NORB), device_id_type=MESH)
-    for d in range(1, NZ):
-        pl.semaphore_signal(barrier, inc=1, device_id=first_peer(d)[1], device_id_type=MESH)
-        pl.semaphore_signal(barrier, inc=1, device_id=second_peer(d)[1], device_id_type=MESH)
+    for k in range(1, NAUX):
+        pl.semaphore_signal(barrier, inc=1, device_id=(sysi, (aux + k) % NAUX, me), device_id_type=MESH)
 
     for j in range(PACK):
         cwt[j] = jnp.zeros((2 * LANES, nbas), F32)
@@ -98,6 +98,9 @@
             trecv[sp, s * SLOT + ml:(s + 1) * SLOT, :] = jnp.zeros((SLOT - ml, NC * lanes), F32)
         for s in range(NY):
             s2[sp, s, HALF - 8:HALF, :] = jnp.zeros((8, WIDE), F32)
+    for a in range(NAUX):
+        jsend[a, HALF - 8:HALF, :] = jnp.zeros((8, LANES), F32)
+    jpad[...] = jnp.zeros(jpad.shape, F32)
     rowsel = jnp.where(iota((ml, nbas), 1) == me * ml + iota((ml, nbas), 0), 1.0, 0.0).astype(F32)
     crow = dot_nt(rowsel, cwt[0] + cwt[1] + cwt[2])
 
@@ -107,16 +110,6 @@
     def t_copy(sp, dest, src):
         return remote(tsend.at[sp, dest], trecv.at[sp, rows_of(src), pl.ds(0, lanes)],
                       ts_sem.at[sp, dest], tr_sem.at[sp, src], orb_dev(dest))
-
-    def relay_in(sp, hh):
-        dest = NC * ((xi + 2) % NX) + hh
-        return remote(tsend.at[sp, dest], rel.at[sp, hh], ts_sem.at[sp, dest], rr_sem.at[sp, hh],
-                      orb_dev(NC * ((xi + step) % NX) + hi))
-
-    def relay_out(sp, hh):
-        src = NC * ((xi + NX - step) % NX) + hi
-        return remote(rel.at[sp, hh], trecv.at[sp, rows_of(src), pl.ds(0, lanes)],
-                      rs_sem.at[sp, hh], tr_sem.at[sp, src], orb_dev(NC * ((xi + step) % NX) + hh))
 
     def share(sp, src):
         return remote(trecv.at[sp, rows_of(src), pl.ds(0, lanes)],
@@ -145,27 +138,24 @@
 
         @pl.when(i == 0)
         def _():
-            pl.semaphore_wait(barrier, NORB - 1 + 2 * (NZ - 1))
+            pl.semaphore_wait(barrier, NORB - 1 + NAUX - 1)
             for sp in range(2):
                 for hh in range(NC):
-                    relay_in(sp, hh).start()
-
-        @pl.when((i == 1) | (i == 2))
+                    t_copy(sp, NC * xp + hh, me).start()
+
+        @pl.when(i == 1)
+        def _():
+            for sp in range(2):
+                t_copy(sp, partner, me).start()
+                share_own(sp).start()
+
+        @pl.when(i == 2)
         def _():
             for hh in range(NC):
                 t_copy(0, NC * xp + hh, me).start()
-
-        @pl.when(i == NX - 1)
-        def _():
-            t_copy(0, partner, me).start()
-            share_own(0).start()
         return 0
 
     lax.fori_loop(0, NX, t_chunk, 0)
-
-    for hh in range(NC):
-        relay_in(0, hh).wait_recv()
-        relay_out(0, hh).start()
 
     ngrp = NX * gpc
     nrow = ngrp // 8
@@ -185,12 +175,12 @@
     for o in range(1, NORB):
         g_copy((me + o) % NORB, me).start()
     grecv[me] = gpart
-    near = [NC * chunk_chip(i) + hh for i in (1, 2) for hh in range(NC)]
-    far = [NC * ((xi + 2) % NX) + hh for hh in range(NC)]
+    near = [NC * chunk_chip(i) + hh for i in (2, 3) for hh in range(NC)]
+    far = [NC * chunk_chip(0) + hh for hh in range(NC)]
+    for dest in near[2:]:
+        t_copy(0, dest, me).start()
     for dest in near:
         t_copy(1, dest, me).start()
-    t_copy(1, partner, me).start()
-    share_own(1).start()
     for sp in range(2):
         trecv[sp, rows_of(me), 0:lanes] = tsend[sp, me]
         trecv[sp, rows_of(me), lanes:2 * lanes] = tsend[sp, partner]
@@ -200,8 +190,8 @@
             t_copy(sp, src, src).wait_recv()
             share(sp, src).start()
 
-    def j_copy():
-        return remote(jown.at[1 - hi], jother, j_sem.at[0], j_sem.at[1], orb_dev(partner))
+    def j_copy(dest, src):
+        return remote(jsend.at[dest], jrecv.at[src], js_sem.at[dest], jr_sem.at[src], (sysi, dest, me))
 
     def p1_copy(sp, d):
         q, dev = first_peer(d)
@@ -239,20 +229,13 @@
             return acc
 
         jmat = lax.fori_loop(0, ngrp, add, jnp.zeros((ml, nbas), F32))
-        col = iota((nbas, NORB * SLOT), 0)
-        spread = jnp.where((col // ml) * SLOT + col % ml == iota((nbas, NORB * SLOT), 1), 1.0, 0.0).astype(F32)
-        wide = dot(jmat, spread)
-        for h in range(NC):
-            jown[h] = wide[:, h * WIDE:(h + 1) * WIDE]
-        j_copy().start()
-        row, r = iota((nbas, ml), 0), iota((nbas, ml), 1)
-        pos = row // cols
-        nat = jnp.where(hi == 0, pos, (pos % NZ) * NY + pos // NZ) * cols + row % cols
-        own = jnp.where(nat == me * ml + r, 1.0, 0.0).astype(F32)
-        other = jnp.where(nat == partner * ml + r, 1.0, 0.0).astype(F32)
-        mine = dot(own, jown[hi])
-        j_copy().wait_recv()
-        jfull[...] = (mine + dot(other, jother[...])).reshape(NZ, NY * cols, WIDE)
+        jpad[0:ml, 0:nbas] = jmat
+        jt = jpad[...].T
+        for a in range(NAUX):
+            jsend[a, 0:cols, :] = jt[a * cols:(a + 1) * cols]
+        for k in range(1, NAUX):
+            j_copy((aux + k) % NAUX, aux).start()
+        jrecv[aux] = jsend[aux]
 
     def exchange(sp):
         for o in range(1, NORB):
@@ -269,7 +252,7 @@
         def rows(c, _):
             r0 = pl.multiple_of(c * (2 * NY * cols), 8)
             prod = dot_nt(tlhs[pl.ds(r0, 2 * NY * cols), :], trecv[sp, rhs, :])
-            kbuf[sp, pl.ds(2 * c, 2)] = jfull[pl.ds(2 * c, 2)] - prod.reshape(2, NY * cols, WIDE)
+            kbuf[sp, pl.ds(2 * c, 2)] = prod.reshape(2, NY * cols, WIDE)
             return 0
 
         lax.fori_loop(0, NZ // 2, rows, 0)
@@ -300,40 +283,40 @@
             def _():
                 r3[sp, xi] = s3[sp, k // NC]
 
-    def finish(sp, o_ref):
+    def finish(sp, o_ref, jtot):
         for x in range(NX):
             @pl.when(NC * x + xi // NC != me)
             def _():
                 p3_wait(sp, x).wait_recv()
         tot = ((r3[sp, 0] + r3[sp, 1]) + r3[sp, 2]) + r3[sp, 3]
         half = jnp.where(hi == 0, tot[:, :SLOT], tot[:, SLOT:])
-        o_ref[...] = half[:cols, :ml]
-
+        o_ref[...] = jtot[:cols, :ml] - half[:cols, :ml]
+
+    pass_on(0, far)
+    pass_on(1, far)
+    for sp in range(2):
+        t_copy(sp, partner, partner).wait_recv()
+    coulomb()
     pass_on(0, near)
-    for hh in range(NC):
-        relay_in(1, hh).wait_recv()
-        relay_out(1, hh).start()
-    pass_on(0, far)
-    t_copy(0, partner, partner).wait_recv()
-    coulomb()
     exchange(0)
     pass_on(1, near)
-    pass_on(1, far)
-    t_copy(1, partner, partner).wait_recv()
     exchange(1)
     stage2(0)
+    stage2(1)
+    for k in range(1, NAUX):
+        src = (aux + k) % NAUX
+        j_copy(src, src).wait_recv()
+    jtot = jrecv[0]
+    for a in range(1, NAUX):
+        jtot = jtot + jrecv[a]
     stage3(0)
-    stage2(1)
     stage3(1)
-    finish(0, oa_ref)
-    finish(1, ob_ref)
+    finish(0, oa_ref, jtot)
+    finish(1, ob_ref, jtot)
 
     for sp in range(2):
-        for dest in near + [partner]:
+        for dest in near + far + [partner]:
             t_copy(sp, dest, me).wait_send()
-        for hh in range(NC):
-            relay_in(sp, hh).wait_send()
-            relay_out(sp, hh).wait_send()
         for src in near + far:
             share(sp, src).wait_send()
         share_own(sp).wait_send()
@@ -346,7 +329,8 @@
                 p3_copy(sp, k).wait_send()
     for o in range(1, NORB):
         g_copy((me + o) % NORB, me).wait_send()
-    j_copy().wait_send()
+    for k in range(1, NAUX):
+        j_copy((aux + k) % NAUX, aux).wait_send()
 
 
 def solution(mesh):
@@ -369,24 +353,23 @@
                 pltpu.VMEM(b4.shape, F32),
                 pltpu.VMEM((PACK, 2 * LANES, nbas), F32),
                 pltpu.VMEM((2, NORB, ml, lanes), F32),
-                pltpu.VMEM((2, NC, ml, lanes), F32),
                 pltpu.VMEM((2, width, NC * lanes), F32),
                 pltpu.VMEM((nbas, NC * lanes), F32),
                 pltpu.VMEM((q_loc // PACK, 2 * LANES), F32),
                 pltpu.VMEM((8, LANES), F32),
                 pltpu.VMEM((NORB, 8, LANES), F32),
                 pltpu.VMEM((q_loc, LANES), F32),
-                pltpu.VMEM((NC, ml, WIDE), F32),
-                pltpu.VMEM((ml, WIDE), F32),
-                pltpu.VMEM((NZ, NY * cols, WIDE), F32),
+                pltpu.VMEM((LANES, width), F32),
+                pltpu.VMEM((NAUX, HALF, LANES), F32),
+                pltpu.VMEM((NAUX, HALF, LANES), F32),
                 pltpu.VMEM((2, NZ, NY * cols, WIDE), F32),
                 pltpu.VMEM((2, NZ - 1, NY * cols, WIDE), F32),
                 pltpu.VMEM((2, NY, HALF, WIDE), F32),
                 pltpu.VMEM((2, NZ - 1, HALF, WIDE), F32),
                 pltpu.VMEM((2, NX // NC, HALF, LANES), F32),
                 pltpu.VMEM((2, NX, HALF, LANES), F32),
-                dma((NX,)), dma((2, NORB)), dma((2, NORB)), dma((2, NC)), dma((2, NC)),
-                dma((2, NORB)), dma((2, NORB)), dma((NORB,)), dma((NORB,)), dma((2,)),
+                dma((NX,)), dma((2, NORB)), dma((2, NORB)),
+                dma((2, NORB)), dma((2, NORB)), dma((NORB,)), dma((NORB,)), dma((NAUX,)), dma((NAUX,)),
                 dma((2, NZ - 1)), dma((2, NZ - 1)), dma((2, NZ - 1)), dma((2, NZ - 1)),
                 dma((2, NX)), dma((2, NX)),
             ],

time: 53.8 us -> 52 us (0.967)
  Pallas kernels: 50.2 us -> 48.5 us
    pallas_call x1, Pallas kernels: 50.2 us -> 48.5 us  [local_build(): pl.pallas_call(functools.partial(kernel, (ng, ml, nbas, na, nb)), out_sha...]
where the time goes in v3:
time: 52 us; the launch traced here: 51.7 us
  Pallas kernels  48.5 us (93%)
  local copies, waits for them, and re-layouts  2.65 us (5%)
  between operations  0.64 us (1%)
    pallas_call x1, Pallas kernels, local_build(): pl.pallas_call(functools.partial(kernel, (ng, ml, nbas, na, nb)), out_sha...  48.5 us
    unnamed x2, local copies, waits for them, and re-layouts  2.65 us

profile of v3, /device:TPU:1, one launch (start us, length us, event | category | flops | bytes accessed | tf_op | source)
XLA Modules:
  0.0 51.7 jit_solution(15177494398499562229)
XLA Ops:
  0.6 48.5 %shard_map.50 = (f32[28,56]{1,0:T(8,128)}, f32[28,56]{1,0:T(8,128)}) custom-call(f32[24,3,56,448]{3,2,1,0:T(8,128)} %bitcast.5, f32[39,448]{1,0:T(8,128)} %bitcast.6, f32[38,448]{1,0:T(8,128)} %bitcast.7), custom_call_target="tpu_custom_call" | custom-call | tf_op jit(solution)/shard_map/pallas_call | solution.py:347
  49.1 1.3 %copy.7 = f32[56,28]{0,1:T(8,128)} copy(f32[56,28]{0,1:T(8,128)} %bitcast.9) | data formatting | bytes 12544
  50.4 1.3 %copy.8 = f32[56,28]{0,1:T(8,128)} copy(f32[56,28]{0,1:T(8,128)} %bitcast.8) | data formatting | bytes 12544

commit v4 on v3

v4 whole, which is shorter than its diff:
```python
import functools

import jax
import jax.numpy as jnp
from jax import lax
from jax.experimental import pallas as pl
from jax.experimental.pallas import tpu as pltpu
from jax.sharding import PartitionSpec as P

TOP_PRECISION = lax.Precision.HIGHEST
F32 = jnp.float32
MESH = pl.DeviceIdType.MESH

NX, NC = 4, 2
NZ, NY = 4, 4
NORB = NX * NC
NAUX = NZ * NY
PACK = 3
LANES = 128
SLOT = 64
HALF = 32
WIDE = NORB * SLOT // NC
NT = (((1,), (1,)), ((), ()))


def dot(a, b):
    return jnp.dot(a, b, precision=TOP_PRECISION, preferred_element_type=F32)


def dot_nt(a, b):
    return lax.dot_general(a, b, NT, precision=TOP_PRECISION, preferred_element_type=F32)


def iota(shape, dim):
    return lax.broadcasted_iota(jnp.int32, shape, dim)


def kernel(dims, b_hbm, ca_hbm, cb_hbm, o_ref,
           bbuf, ca_ref, cb_ref, cwt, tsend, trecv, tlhs, pbuf, gsend, grecv, gam, jpad, jsend, jrecv,
           kbuf, r1, s2, r2, s3, r3,
           b_sem, c_sem, ts_sem, tr_sem, ps_sem, pr_sem, gs_sem, gr_sem, js_sem, jr_sem,
           s1_sem, r1_sem, s2_sem, r2_sem, s3_sem, r3_sem):
    ng, ml, nbas, na, nb = dims
    cols = nbas // (NZ * NY)
    aux = lax.axis_index("aux")
    me = lax.axis_index("orb")
    sysi = lax.axis_index("sys")
    xi, hi = me // NC, me % NC
    zi, yi = aux // NY, aux % NY
    partner = me + 1 - 2 * hi
    step = 1 + 2 * hi
    p_idx = jnp.where(hi == 0, zi, yi)
    s_idx = jnp.where(hi == 0, yi, zi)
    p_stride = jnp.where(hi == 0, NY, 1)
    s_stride = jnp.where(hi == 0, 1, NY)

    def first_peer(d):
        q = (p_idx + d) % NZ
        return q, (sysi, q * p_stride + s_idx * s_stride, me)

    def second_peer(d):
        q = (s_idx + d) % NZ
        return q, (sysi, p_idx * p_stride + q * s_stride, me)

    def orb_dev(o):
        return (sysi, aux, o)

    def remote(src, dst, send, recv, dev):
        return pltpu.make_async_remote_copy(src_ref=src, dst_ref=dst, send_sem=send, recv_sem=recv,
                                            device_id=dev, device_id_type=MESH)

    gpc = NC * ng

    def chip_of(i):
        off = jnp.where(i == 0, 2, jnp.where(i == 1, step, jnp.where(i == 2, NX - step, 0)))
        return (xi + off) % NX

    far, side, back = ([NC * chip_of(i) + hh for hh in range(NC)] for i in range(3))
    near = side + back

    def b_copy(i):
        part = pl.ds(chip_of(i) * gpc, gpc)
        return pltpu.make_async_copy(b_hbm.at[part], bbuf.at[part], b_sem.at[i])

    b_copy(0).start()
    c_copies = [pltpu.make_async_copy(ca_hbm, ca_ref, c_sem.at[0]), pltpu.make_async_copy(cb_hbm, cb_ref, c_sem.at[1])]
    for c in c_copies:
        c.start()
    for i in range(1, NX):
        b_copy(i).start()

    barrier = pltpu.get_barrier_semaphore()
    for o in range(1, NORB):
        pl.semaphore_signal(barrier, inc=1, device_id=orb_dev((me + o) % NORB), device_id_type=MESH)
    for k in range(1, NAUX):
        pl.semaphore_signal(barrier, inc=1, device_id=(sysi, (aux + k) % NAUX, me), device_id_type=MESH)

    for sp in range(2):
        for g in range(ng):
            for s in range(NORB):
                trecv[sp, g, s * SLOT + ml:(s + 1) * SLOT, :] = jnp.zeros((SLOT - ml, NC * LANES), F32)
        for s in range(NY):
            s2[sp, s, HALF - 8:HALF, :] = jnp.zeros((8, WIDE), F32)
    for a in range(NAUX):
        jsend[a, HALF - 8:HALF, :] = jnp.zeros((8, LANES), F32)
    jpad[...] = jnp.zeros(jpad.shape, F32)
    for j in range(PACK):
        cwt[j] = jnp.zeros((2 * LANES, nbas), F32)
    for c in c_copies:
        c.wait()
    for j in range(PACK):
        cwt[j, na * j:na * (j + 1), :] = ca_ref[...]
        cwt[j, LANES + nb * j:LANES + nb * (j + 1), :] = cb_ref[...]
    rowsel = jnp.where(iota((ml, nbas), 1) == me * ml + iota((ml, nbas), 0), 1.0, 0.0).astype(F32)
    crow = dot_nt(rowsel, cwt[0] + cwt[1] + cwt[2])

    def rows_of(src):
        return pl.ds(pl.multiple_of(src * SLOT, SLOT), ml)

    def t_copy(sp, dest, src, g=None):
        part = pl.ds(0, ng) if g is None else g
        k = 0 if g is None else g
        return remote(tsend.at[sp, dest, part], trecv.at[sp, part, rows_of(src), pl.ds(0, LANES)],
                      ts_sem.at[sp, dest, k], tr_sem.at[sp, src, k], orb_dev(dest))

    def share(sp, src, g=None):
        part = pl.ds(0, ng) if g is None else g
        k = 0 if g is None else g
        return remote(trecv.at[sp, part, rows_of(src), pl.ds(0, LANES)],
                      trecv.at[sp, part, rows_of(src), pl.ds(LANES, LANES)],
                      ps_sem.at[sp, src, k], pr_sem.at[sp, src, k], orb_dev(partner))

    def share_own(sp):
        return remote(tsend.at[sp, me], trecv.at[sp, pl.ds(0, ng), rows_of(me), pl.ds(LANES, LANES)],
                      ps_sem.at[sp, me, 0], pr_sem.at[sp, me, 0], orb_dev(partner))

    def t_chunk(i, _):
        chip = chip_of(i)
        b_copy(i).wait()
        acc = None
        for j in range(PACK):
            part = dot_nt(bbuf[pl.ds(chip * gpc, gpc), j].reshape(gpc * ml, nbas), cwt[j])
            acc = part if acc is None else acc + part
        for k in range(gpc):
            blk = acc[k * ml:(k + 1) * ml]
            tsend[0, NC * chip + k // ng, k % ng] = blk[:, :LANES]
            tsend[1, NC * chip + k // ng, k % ng] = blk[:, LANES:]
            pbuf[pl.ds(chip * gpc + k, 1), :] = jnp.sum(blk * crow, axis=0, keepdims=True)

        @pl.when(i == 0)
        def _():
            pl.semaphore_wait(barrier, NORB - 1 + NAUX - 1)

        @pl.when(i < NX - 1)
        def _():
            for hh in range(NC):
                t_copy(0, NC * chip + hh, me).start()
        return 0

    lax.fori_loop(0, NX, t_chunk, 0)
    for sp in range(2):
        t_copy(sp, partner, me).start()
        share_own(sp).start()

    ngrp = NORB * ng
    nrow = ngrp // 8
    lane = iota((8, LANES), 1)
    gpart = jnp.zeros((8, LANES), F32)
    for r in range(nrow):
        pa = pbuf[8 * r:8 * r + 8, 0:LANES]
        pb = pbuf[8 * r:8 * r + 8, LANES:2 * LANES]
        for j in range(PACK):
            part = (jnp.where((lane >= na * j) & (lane < na * (j + 1)), pa, 0.0)
                    + jnp.where((lane >= nb * j) & (lane < nb * (j + 1)), pb, 0.0))
            gpart = jnp.where(lane == PACK * r + j, jnp.sum(part, axis=1, keepdims=True), gpart)
    gsend[...] = gpart

    def g_copy(dest, src):
        return remote(gsend, grecv.at[src], gs_sem.at[dest], gr_sem.at[src], orb_dev(dest))

    for o in range(1, NORB):
        g_copy((me + o) % NORB, me).start()
    grecv[me] = gpart
    for dest in far:
        t_copy(1, dest, me).start()
    for g in range(ng):
        for dest in near:
            t_copy(1, dest, me, g).start()
    for sp in range(2):
        trecv[sp, :, rows_of(me), 0:LANES] = tsend[sp, me]
        trecv[sp, :, rows_of(me), LANES:2 * LANES] = tsend[sp, partner]

    def pass_on(sp, sources, g=None):
        for src in sources:
            t_copy(sp, src, src, g).wait_recv()
            share(sp, src, g).start()

    def shared(sp, sources, g=None):
        for src in sources:
            share(sp, src, g).wait_recv()

    def j_copy(dest, src):
        return remote(jsend.at[dest], jrecv.at[src], js_sem.at[dest], jr_sem.at[src], (sysi, dest, me))

    def p1_copy(sp, d):
        q, dev = first_peer(d)
        return remote(kbuf.at[sp, q], r1.at[sp, d - 1], s1_sem.at[sp, d - 1], r1_sem.at[sp, d - 1], dev)

    def p2_copy(sp, d):
        q, dev = second_peer(d)
        return remote(s2.at[sp, q], r2.at[sp, d - 1], s2_sem.at[sp, d - 1], r2_sem.at[sp, d - 1], dev)

    def p3_copy(sp, k):
        return remote(s3.at[sp, k // NC], r3.at[sp, xi], s3_sem.at[sp, k], r3_sem.at[sp, xi],
                      orb_dev(NX * hi + k))

    def p3_wait(sp, x):
        return remote(s3.at[sp, 0], r3.at[sp, x], s3_sem.at[sp, 0], r3_sem.at[sp, x],
                      orb_dev(NC * x + xi // NC))

    def coulomb():
        for o in range(1, NORB):
            src = (me + o) % NORB
            g_copy(src, src).wait_recv()
        gsum = grecv[0]
        for s in range(1, NORB):
            gsum = gsum + grecv[s]
        for r in range(nrow):
            for j in range(PACK):
                c = PACK * r + j
                gam[c * 8:c * 8 + 8, :] = jnp.broadcast_to(gsum[:, c:c + 1], (8, LANES))

        nblk = pl.cdiv(nbas, LANES)
        ends = [(k * LANES, min(nbas, (k + 1) * LANES)) for k in range(nblk)]

        def add(g, acc):
            r, row = g // 8, g % 8
            for j in range(PACK):
                w = gam[pl.ds((PACK * r + j) * 8 + row, 1), :]
                acc = tuple(a + bbuf[g, j, :, lo:hi_] * w[:, :hi_ - lo] for a, (lo, hi_) in zip(acc, ends))
            return acc

        jmat = lax.fori_loop(0, ngrp, add, tuple(jnp.zeros((ml, hi_ - lo), F32) for lo, hi_ in ends))
        for a, (lo, hi_) in zip(jmat, ends):
            jpad[0:ml, lo:hi_] = a
        jt = jpad[...].T
        for a in range(NAUX):
            jsend[a, 0:cols, :] = jt[a * cols:(a + 1) * cols]
        for k in range(1, NAUX):
            j_copy((aux + k) % NAUX, aux).start()
        jrecv[aux] = jsend[aux]

    def k_step(sp, g):
        for h in range(NC):
            @pl.when(hi == h)
            def _():
                for a in range(NZ * NY):
                    at = a if h == 0 else (a % NY) * NZ + a // NY
                    base = (a // 2) * SLOT + (a % 2) * cols
                    tlhs[at * cols:(at + 1) * cols, :] = trecv[sp, g, base:base + cols, :]
        rhs = pl.ds(pl.multiple_of(WIDE * hi, WIDE), WIDE)
        prod = dot_nt(tlhs[...], trecv[sp, g, rhs, :]).reshape(NZ, NY * cols, WIDE)
        kbuf[sp] = kbuf[sp] + prod

    def k_send(sp):
        for d in (2, 1, 3):
            p1_copy(sp, d).start()

    def stage2(sp):
        for d in (1, 3, 2):
            p1_copy(sp, d).wait_recv()
        tot = ((kbuf[sp, p_idx] + r1[sp, 0]) + r1[sp, 1]) + r1[sp, 2]
        for s in range(NY):
            s2[sp, s, 0:cols, :] = tot[s * cols:(s + 1) * cols]
        for d in (2, 1, 3):
            p2_copy(sp, d).start()

    def stage3(sp):
        for d in (1, 3, 2):
            p2_copy(sp, d).wait_recv()
        tot = ((s2[sp, s_idx] + r2[sp, 0]) + r2[sp, 1]) + r2[sp, 2]
        for x in range(NX // NC):
            s3[sp, x] = tot[:, x * LANES:(x + 1) * LANES]
        for k in range(NX):
            @pl.when(NX * hi + k != me)
            def _():
                p3_copy(sp, k).start()

            @pl.when(NX * hi + k == me)
            def _():
                r3[sp, xi] = s3[sp, k // NC]

    def finish(sp, jtot):
        for x in range(NX):
            @pl.when(NC * x + xi // NC != me)
            def _():
                p3_wait(sp, x).wait_recv()
        tot = ((r3[sp, 0] + r3[sp, 1]) + r3[sp, 2]) + r3[sp, 3]
        half = jnp.where(hi == 0, tot[:, :SLOT], tot[:, SLOT:])
        o_ref[sp] = jtot[:cols, :ml] - half[:cols, :ml]

    kbuf[...] = jnp.zeros(kbuf.shape, F32)
    for sp in range(2):
        t_copy(sp, partner, partner).wait_recv()
    pass_on(0, far)
    pass_on(0, near)
    coulomb()
    shared(0, far + near + [partner])

    def alpha_step(g, _):
        k_step(0, g)
        return 0

    lax.fori_loop(0, ng, alpha_step, 0)
    k_send(0)
    pass_on(1, far)
    shared(1, far + [partner])
    pass_on(1, near, 0)

    def beta_step(g, _):
        @pl.when(g < ng - 1)
        def _():
            pass_on(1, near, g + 1)
        shared(1, near, g)
        k_step(1, g)
        return 0

    lax.fori_loop(0, ng, beta_step, 0)
    k_send(1)
    stage2(0)
    stage2(1)
    for k in range(1, NAUX):
        src = (aux + k) % NAUX
        j_copy(src, src).wait_recv()
    jtot = jrecv[0]
    for a in range(1, NAUX):
        jtot = jtot + jrecv[a]
    stage3(0)
    stage3(1)
    finish(0, jtot)
    finish(1, jtot)

    for sp in range(2):
        for g in (range(ng) if sp else (None,)):
            for dest in near:
                t_copy(sp, dest, me, g).wait_send()
                share(sp, dest, g).wait_send()
        for dest in far:
            t_copy(sp, dest, me).wait_send()
            share(sp, dest).wait_send()
        t_copy(sp, partner, me).wait_send()
        share_own(sp).wait_send()
        for d in range(1, NZ):
            p1_copy(sp, d).wait_send()
            p2_copy(sp, d).wait_send()
        for k in range(NX):
            @pl.when(NX * hi + k != me)
            def _():
                p3_copy(sp, k).wait_send()
    for o in range(1, NORB):
        g_copy((me + o) % NORB, me).wait_send()
    for k in range(1, NAUX):
        j_copy((aux + k) % NAUX, aux).wait_send()


def solution(mesh):
    def local_build(b_local, c_alpha, c_beta):
        q_loc, ml, nbas = b_local.shape
        na, nb = c_alpha.shape[1], c_beta.shape[1]
        ng = q_loc // (PACK * NORB)
        b4 = b_local.reshape(q_loc // PACK, PACK, ml, nbas)
        width = NORB * SLOT
        cols = nbas // (NZ * NY)
        dma = pltpu.SemaphoreType.DMA
        vmem = pl.BlockSpec(memory_space=pltpu.VMEM)
        out = pl.pallas_call(
            functools.partial(kernel, (ng, ml, nbas, na, nb)),
            out_shape=jax.ShapeDtypeStruct((2, cols, ml), F32),
            in_specs=[pl.BlockSpec(memory_space=pl.ANY)] * 3,
            out_specs=vmem,
            scratch_shapes=[
                pltpu.VMEM(b4.shape, F32),
                pltpu.VMEM((na, nbas), F32),
                pltpu.VMEM((nb, nbas), F32),
                pltpu.VMEM((PACK, 2 * LANES, nbas), F32),
                pltpu.VMEM((2, NORB, ng, ml, LANES), F32),
                pltpu.VMEM((2, ng, width, NC * LANES), F32),
                pltpu.VMEM((nbas, NC * LANES), F32),
                pltpu.VMEM((q_loc // PACK, 2 * LANES), F32),
                pltpu.VMEM((8, LANES), F32),
                pltpu.VMEM((NORB, 8, LANES), F32),
                pltpu.VMEM((q_loc, LANES), F32),
                pltpu.VMEM((LANES, width), F32),
                pltpu.VMEM((NAUX, HALF, LANES), F32),
                pltpu.VMEM((NAUX, HALF, LANES), F32),
                pltpu.VMEM((2, NZ, NY * cols, WIDE), F32),
                pltpu.VMEM((2, NZ - 1, NY * cols, WIDE), F32),
                pltpu.VMEM((2, NY, HALF, WIDE), F32),
                pltpu.VMEM((2, NZ - 1, HALF, WIDE), F32),
                pltpu.VMEM((2, NX // NC, HALF, LANES), F32),
                pltpu.VMEM((2, NX, HALF, LANES), F32),
                dma((NX,)), dma((2,)), dma((2, NORB, ng)), dma((2, NORB, ng)),
                dma((2, NORB, ng)), dma((2, NORB, ng)), dma((NORB,)), dma((NORB,)), dma((NAUX,)), dma((NAUX,)),
                dma((2, NZ - 1)), dma((2, NZ - 1)), dma((2, NZ - 1)), dma((2, NZ - 1)),
                dma((2, NX)), dma((2, NX)),
            ],
            compiler_params=pltpu.CompilerParams(
                collective_id=0, has_side_effects=True, vmem_limit_bytes=60 * 1024 * 1024),
        )(b4, c_alpha.T, c_beta.T)
        return out[0].T, out[1].T

    spec_b = P(('sys', 'aux'), 'orb', None)
    spec_c = P('sys', None)
    spec_g = P(('sys', 'orb'), 'aux')
    return jax.shard_map(local_build, mesh=mesh, in_specs=(spec_b, spec_c, spec_c), out_specs=(spec_g, spec_g), check_vma=False)
```

time: 52 us -> 49.6 us (0.954)
  local copies, waits for them, and re-layouts: 2.65 us -> 1.35 us
  Pallas kernels: 48.5 us -> 47.4 us
    unnamed x2 -> x0, local copies, waits for them, and re-layouts: 2.65 us -> none
    transpose x0 -> x1, local copies, waits for them, and re-layouts: none -> 1.35 us  [local_build(): return (out[0].T, out[1].T)]
    pallas_call x1, Pallas kernels: 48.5 us -> 47.4 us  [local_build(): pl.pallas_call(functools.partial(kernel, (ng, ml, nbas, na, nb)), out_sha...]
where the time goes in v4:
time: 49.6 us; the launch traced here: 49.4 us
  Pallas kernels  47.4 us (96%)
  local copies, waits for them, and re-layouts  1.35 us (3%)
  between operations  0.64 us (1%)
    pallas_call x1, Pallas kernels, local_build(): pl.pallas_call(functools.partial(kernel, (ng, ml, nbas, na, nb)), out_sha...  47.4 us
    transpose x1, local copies, waits for them, and re-layouts, local_build(): return (out[0].T, out[1].T)  1.35 us

profile of v4, /device:TPU:1, one launch (start us, length us, event | category | flops | bytes accessed | tf_op | source)
XLA Modules:
  0.0 49.4 jit_solution(14656499487405521440)
XLA Ops:
  0.6 47.4 %shard_map.50 = f32[2,28,56]{2,1,0:T(8,128)} custom-call(f32[24,3,56,448]{3,2,1,0:T(8,128)} %bitcast.11, f32[39,448]{1,0:T(8,128)} %bitcast.12, f32[38,448]{1,0:T(8,128)} %bitcast.13), custom_call_target="tpu_custom_call" | custom-call | tf_op jit(solution)/shard_map/pallas_call | solution.py:376
  48.1 1.3 %slice_bitcast_fusion = (f32[56,28]{0,1:T(8,128)}, f32[56,28]{0,1:T(8,128)}) fusion(f32[2,28,56]{2,1,0:T(8,128)} %shard_map.50), kind=kLoop, calls=%fused_computation | loop fusion | bytes 25088 | tf_op jit(solution)/shard_map/transpose | solution.py:410
